TPU v7x, 128 devices: a whole 4x4x4 slice. The times are simulated.
128 devices in a mesh: section: 4 (over x), fsdp: 32 (over y, z, core).
Axes of the slice: x: 4, y: 4, z: 4, core: 2. Of those that a mesh axis runs over, the one named last changes fastest.
Arguments:
- grad_parts: bfloat16 [4, 32, 8192, 1024], P('section', 'fsdp'), may hold values from -510 to 510
- first_codes: int32 [4, 8192, 1024], P('section', 'fsdp'), may hold values from -7 to 7
- first_rows: float32 [4, 8192], P('section', 'fsdp'), may hold values from 0.003 to 0.03
- first_columns: float32 [4, 1024], P('section'), may hold values from 0.003 to 0.03
- second_codes: int32 [4, 8192, 1024], P('section', 'fsdp'), may hold values from 1 to 15
- second_rows: float32 [4, 8192], P('section', 'fsdp'), may hold values from 0.001 to 0.01
- second_columns: float32 [4, 1024], P('section'), may hold values from 0.001 to 0.01
Outputs:
- direction: float32 [4, 8192, 1024], P('section', 'fsdp')
- first_scaled: float32 [4, 8192, 1024], P('section', 'fsdp')
- second_scaled: float32 [4, 8192, 1024], P('section', 'fsdp')
- first_rowmax: float32 [4, 8192], P('section', 'fsdp')
- first_colmax: float32 [4, 1024], P('section')
- second_rowmax: float32 [4, 8192], P('section', 'fsdp')
- second_colmax: float32 [4, 1024], P('section')
All inputs are finite; a program needn't handle non-finite values. Where the computation divides by a largest or mean magnitude, that divisor is 1e-20 or more.
Results may differ from a plain program's by a relative error of at most 0.0003.
Values may be sent and summed in bfloat16 or wider, within the bound.
A program may use at most 192 MiB of HBM per device.

v0:
```python
import math

import jax
import jax.numpy as jnp
from jax import lax
from jax.sharding import Mesh
from jax.sharding import PartitionSpec as P

FSDP = ("fsdp_0", "fsdp_1", "fsdp_2")
SECTION_FSDP = ("section", "fsdp_0", "fsdp_1", "fsdp_2")


beta_first = 0.9
beta_second = 0.999
clip_rms = 3.0
epsilon = 1e-08
scale_floor = 0.001


def in_blocks(value, dim, length):
    before, after = (value.shape[:dim], value.shape[dim + 1 :])
    return jnp.moveaxis(value.reshape(*before, length, -1, *after), dim, 0)


def sum_by_chip(value, chips, core, dim):
    sizes = (lax.axis_size(chips), lax.axis_size(core))
    parts = in_blocks(value, dim, sizes[0] * sizes[1])
    inside = parts.shape[1:]
    parts = parts.reshape(*sizes, *inside).swapaxes(0, 1).reshape(-1, *inside)
    parts = lax.psum_scatter(parts, core, scatter_dimension=0, tiled=True)
    return lax.psum_scatter(parts, chips, scatter_dimension=0, tiled=True)[0]


def by_axis(value, axes):
    for axis in axes:
        value = lax.psum(value, axis)
    return value


def copy_for_each(value, axis):
    copies = jnp.broadcast_to(value, (lax.axis_size(axis), *value.shape))
    return lax.all_to_all(copies, axis, split_axis=0, concat_axis=0, tiled=True)


def of_everyone(value, axis):
    everything = copy_for_each(value, axis)
    return jnp.max(everything, axis=0)


def in_one(arrays, axis):
    flat, at, outs = (jnp.concatenate([a.reshape(-1) for a in arrays]), 0, [])
    total = of_everyone(flat, axis)
    for a in arrays:
        outs.append(total[at : at + a.size].reshape(a.shape))
        at += a.size
    return tuple(outs)


def dequantize(code_values, levels, row_scale, col_scale):
    scale_bound = jnp.minimum(row_scale[:, :, None], col_scale[:, None, :])
    return code_values.astype(jnp.float32) / levels * scale_bound


def moments(
    gradient,
    clip_scale,
    first_codes,
    first_rows,
    first_columns,
    second_codes,
    second_rows,
    second_columns,
):
    first_old = dequantize(first_codes, 7.0, first_rows, first_columns)
    second_old = dequantize(second_codes, 15.0, second_rows, second_columns)
    clipped = clip_scale * gradient
    first_new = beta_first * first_old + (1.0 - beta_first) * clipped
    second_new = beta_second * second_old + (1.0 - beta_second) * clipped * clipped
    direction = first_new / (jnp.sqrt(second_new) + epsilon)
    return (first_new, second_new, direction)


def local(
    grad_parts, first_codes, first_rows, first_columns, second_codes, second_rows, second_columns
):
    layer_count = grad_parts.shape[0]
    row_count = grad_parts.shape[2]
    col_count = grad_parts.shape[3]
    entries = layer_count * lax.axis_size("section") * row_count * col_count
    summands = grad_parts.reshape(layer_count, row_count, col_count).astype(jnp.float32)
    gradient = sum_by_chip(summands, ("fsdp_0", "fsdp_1"), "fsdp_2", 1)
    square_sum = by_axis(jnp.sum(gradient * gradient), SECTION_FSDP)
    clip_limit = clip_rms * math.sqrt(entries)
    clip_scale = clip_limit / jnp.maximum(jnp.sqrt(square_sum), clip_limit)
    first_new, second_new, direction = moments(
        gradient,
        clip_scale,
        first_codes,
        first_rows,
        first_columns,
        second_codes,
        second_rows,
        second_columns,
    )
    first_rowmax = jnp.maximum(jnp.max(jnp.abs(first_new), axis=2), scale_floor)
    first_local = jnp.max(jnp.abs(first_new), axis=1)
    second_rowmax = jnp.max(second_new, axis=2)
    second_local = jnp.max(second_new, axis=1)
    first_colmax, second_colmax = in_one((first_local, second_local), FSDP)
    first_colmax = jnp.maximum(first_colmax, scale_floor)
    first_scaled = first_new / jnp.minimum(first_rowmax[:, :, None], first_colmax[:, None, :])
    second_scaled = second_new / jnp.minimum(second_rowmax[:, :, None], second_colmax[:, None, :])
    return (
        direction,
        first_scaled,
        second_scaled,
        first_rowmax,
        first_colmax,
        second_rowmax,
        second_colmax,
    )


def solution(mesh):
    torus = Mesh(
        mesh.devices.reshape(mesh.shape["section"], 4, 4, 2),
        ("section", "fsdp_0", "fsdp_1", "fsdp_2"),
    )
    placed = (
        P("section", FSDP, None, None),
        P("section", FSDP, None),
        P("section", FSDP),
        P("section", None),
        P("section", FSDP, None),
        P("section", FSDP),
        P("section", None),
    )
    return jax.shard_map(
        local,
        mesh=torus,
        in_specs=placed,
        out_specs=(
            P("section", FSDP, None),
            P("section", FSDP, None),
            P("section", FSDP, None),
            P("section", FSDP),
            P("section", None),
            P("section", FSDP),
            P("section", None),
        ),
        check_vma=False,
    )
```

profile of v0, /device:TPU:1, one launch (start us, length us, event | category | flops | bytes accessed | tf_op | source)
XLA Modules:
  0.0 253.1 jit_solution(7152842142712319265)
XLA Ops:
  7.2 0.0 reduce-scatter.5.cloned.1.call-start
  7.2 18.6 %copy.17 = f32[16,2,1,256,1024]{4,3,0,1,2:T(8,128)} copy(bf16[16,2,1,256,1024]{4,3,1,0,2:T(8,128)(2,1)} %bitcast.22) | data formatting | bytes 50331648 | tf_op jit(solution)/shard_map/reshape | solution.py:29
  25.8 0.0 reduce-scatter.5.cloned.1.call-update
  25.8 0.0 copy-start
  25.8 0.0 copy-start.3
  25.9 0.0 copy-start.4
  25.9 0.0 copy-start.7
  25.9 0.0 copy-start.8
  25.9 0.0 reduce-scatter.7.cloned.1.call-start
  25.9 48.8 %reduce-scatter.5.cloned.1.call-done = f32[16,1,256,1024]{3,2,1,0:T(8,128)} async-done(((f32[32,1,256,1024]{3,2,1,0:T(8,128)}), f32[16,1,256,1024]{3,2,1,0:T(8,128)}) %reduce-scatter.5.cloned.1.call-update) | async-done | bytes 16777232 | tf_op jit(solution)/shard_map/reduce_scatter | solution.py:30
  74.7 0.0 reduce-scatter.7.cloned.1.call-update
  74.8 115.1 %reduce-scatter.7.cloned.1.call-done = f32[1,1,256,1024]{3,2,1,0:T(8,128)} async-done(((f32[16,1,256,1024]{3,2,1,0:T(8,128)}), f32[1,1,256,1024]{3,2,1,0:T(8,128)}) %reduce-scatter.7.cloned.1.call-update) | async-done | bytes 1048592
  189.8 2.1 multiply_reduce_fusion
  191.9 9.1 %psum.28 = f32[]{:T(128)} all-reduce(f32[]{:T(128)} %multiply_reduce_fusion), channel_id=1, replica_groups=mesh['section'=4,'fsdp_0'=4,'fsdp_1'=4,'fsdp_2'=2] {'section'}, use_global_device_ids=true, to_apply=%region_3.0 | all-reduce | flops 1 | bytes 8 | tf_op jit(solution)/shard_map/psum | solution.py:36
  201.0 8.9 %psum.29 = f32[]{:T(128)} all-reduce(f32[]{:T(128)} %psum.28), channel_id=1, replica_groups=mesh['section'=4,'fsdp_0'=4,'fsdp_1'=4,'fsdp_2'=2] {'fsdp_0'}, use_global_device_ids=true, to_apply=%region_4.0 | all-reduce | flops 1 | bytes 8 | tf_op jit(solution)/shard_map/psum | solution.py:36
  209.9 7.1 %psum.30 = f32[]{:T(128)} all-reduce(f32[]{:T(128)} %psum.29), channel_id=1, replica_groups=mesh['section'=4,'fsdp_0'=4,'fsdp_1'=4,'fsdp_2'=2] {'fsdp_1'}, use_global_device_ids=true, to_apply=%region_5.0 | all-reduce | flops 1 | bytes 8 | tf_op jit(solution)/shard_map/psum | solution.py:36
  217.0 9.7 %psum.31 = f32[]{:T(128)} all-reduce(f32[]{:T(128)} %psum.30), channel_id=1, replica_groups=mesh['section'=4,'fsdp_0'=4,'fsdp_1'=4,'fsdp_2'=2] {'fsdp_2'}, use_global_device_ids=true, to_apply=%region_6.0 | all-reduce | flops 1 | bytes 8 | tf_op jit(solution)/shard_map/psum | solution.py:36
  227.4 0.0 copy-done
  227.4 0.0 copy-done.3
  227.4 0.0 copy-done.4
  227.4 0.0 copy-done.7
  227.5 2.5 fusion.2
  229.9 0.0 copy-start.5
  230.0 0.8 broadcast_in_dim.2
  230.8 3.9 %all-to-all-start = ((f32[32,1,2048]{2,1,0:T(1,128)}), f32[32,1,2048]{2,1,0:T(1,128)S(1)}, u32[]{:S(2)}, u32[]{:S(2)}) async-start(f32[32,1,2048]{2,1,0:T(1,128)} %broadcast_in_dim.2), calls=%async_computation.1 | async-start | bytes 524288 | tf_op jit(solution)/shard_map/all_to_all | solution.py:42
  234.7 0.0 copy-start.6
  234.7 9.0 %all-to-all-done = f32[32,1,2048]{2,1,0:T(1,128)S(1)} async-done(((f32[32,1,2048]{2,1,0:T(1,128)}), f32[32,1,2048]{2,1,0:T(1,128)S(1)}, u32[]{:S(2)}, u32[]{:S(2)}) %all-to-all-start) | async-done | bytes 262176 | tf_op jit(solution)/shard_map/all_to_all | solution.py:42
  243.7 0.2 reduce_max.50
  243.9 0.0 copy-start.1
  243.9 0.0 copy-start.2
  243.9 2.3 minimum_divide_fusion
  246.2 0.0 copy-done.1
  (7 shorter events, 0.0 us)
Async XLA Ops:
  7.2 67.6 %reduce-scatter.5.cloned.1.call-start = ((), (), s32[]{:S(2)}) async-start(), calls=%async_computation.3 | async-start | bytes 50331648 | tf_op jit(solution)/shard_map/reduce_scatter | solution.py:30
  25.8 201.6 %copy-start = (s32[1,256,1024]{2,1,0:T(8,128)S(1)}, s32[1,256,1024]{2,1,0:T(8,128)}, u32[]{:S(2)}) copy-start(s32[1,256,1024]{2,1,0:T(8,128)} %param.11) | copy-start | bytes 3145732
  25.8 201.6 %copy-start.3 = (f32[1,1024]{1,0:T(1,128)S(1)}, f32[1,1024]{1,0:T(1,128)}, u32[]{:S(2)}) copy-start(f32[1,1024]{1,0:T(1,128)} %param.13) | copy-start | bytes 12292
  25.9 201.6 %copy-start.4 = (f32[1,1024]{1,0:T(1,128)S(1)}, f32[1,1024]{1,0:T(1,128)}, u32[]{:S(2)}) copy-start(f32[1,1024]{1,0:T(1,128)} %param.10) | copy-start | bytes 12292
  25.9 201.6 %copy-start.7 = (f32[1,256]{1,0:T(1,128)S(1)}, f32[1,256]{1,0:T(1,128)}, u32[]{:S(2)}) copy-start(f32[1,256]{1,0:T(1,128)} %param.12) | copy-start | bytes 3076
  25.9 201.6 %copy-start.8 = (f32[1,256]{1,0:T(1,128)S(1)}, f32[1,256]{1,0:T(1,128)}, u32[]{:S(2)}) copy-start(f32[1,256]{1,0:T(1,128)} %param.9) | copy-start | bytes 3076
  25.9 164.0 %reduce-scatter.7.cloned.1.call-start = ((), (), s32[]{:S(2)}) async-start(), calls=%async_computation.4 | async-start | bytes 17825792
  229.9 16.3 %copy-start.5 = (f32[256]{0:T(256)}, f32[256]{0:T(256)S(1)}, u32[]{:S(2)}) copy-start(f32[256]{0:T(256)S(1)} %get-tuple-element.7) | copy-start | bytes 3076
  230.8 12.9 %all-to-all-start = ((f32[32,1,2048]{2,1,0:T(1,128)}), f32[32,1,2048]{2,1,0:T(1,128)S(1)}, u32[]{:S(2)}, u32[]{:S(2)}) async-start(f32[32,1,2048]{2,1,0:T(1,128)} %broadcast_in_dim.2), calls=%async_computation.1 | async-start | bytes 524288 | tf_op jit(solution)/shard_map/all_to_all | solution.py:42
  234.7 11.5 %copy-start.6 = (f32[256]{0:T(256)}, f32[256]{0:T(256)S(1)}, u32[]{:S(2)}) copy-start(f32[256]{0:T(256)S(1)} %broadcast_maximum_fusion) | copy-start | bytes 3076
  243.9 2.3 copy-start.1
  243.9 2.3 copy-start.2
Sparse Core Ops, SparseCore 0:
  26.0 48.7 reduce-scatter.4
  78.1 111.6 reduce-scatter.6
where the time goes:
time: 254 us; the launch traced here: 253 us
  waiting for transfers between devices  173 us (68%)
  blocking collectives  34.7 us (14%)
  local copies, waits for them, and re-layouts  19.5 us (8%)
  between operations  14.9 us (6%)
  other arithmetic  7.02 us (3%)
  starting transfers between devices  3.94 us (2%)
    unnamed x3, waiting for transfers between devices  115 us
    reduce_scatter x1, waiting for transfers between devices, sum_by_chip(): parts = lax.psum_scatter(parts, core, scatter_dimension=0, tiled=True)  48.8 us
    psum x4, blocking collectives, by_axis(): value = lax.psum(value, axis)  34.7 us
    reshape x1, local copies, waits for them, and re-layouts, sum_by_chip(): parts = parts.reshape(*sizes, *inside).swapaxes(0, 1).reshape(-1, *inside)  18.6 us
    all_to_all x1, waiting for transfers between devices, copy_for_each(): return lax.all_to_all(copies, axis, split_axis=0, concat_axis=0, tiled=True)  9.05 us
  transfers between devices with their start and end apart: 3, of which 3 were waited for; matrix products, arithmetic and copies ran while one was open for 0% of the time, Pallas kernels for 0%

commit v1 on v0

v1 whole, which is shorter than its diff:
```python
import functools
import math

import jax
import jax.numpy as jnp
from jax import lax
from jax.experimental import pallas as pl
from jax.experimental.pallas import tpu as pltpu
from jax.sharding import Mesh
from jax.sharding import PartitionSpec as P

Y, Z, C, X = "fsdp_0", "fsdp_1", "fsdp_2", "section"
FSDP = (Y, Z, C)
MESH = pl.DeviceIdType.MESH

beta_first = 0.9
beta_second = 0.999
clip_rms = 3.0
epsilon = 1e-08
scale_floor = 0.001

SLICES = 8
DIRS = ((0, 1), (1, 3))


def remote(src, dst, send, recv, device):
    return pltpu.make_async_remote_copy(
        src_ref=src, dst_ref=dst, send_sem=send, recv_sem=recv,
        device_id=device, device_id_type=MESH,
    )


def landed(buf, sem):
    pltpu.make_async_copy(buf, buf, sem).wait()


def kernel(
    clip_limit,
    grads, first_codes, first_rows, first_columns, second_codes, second_rows, second_columns,
    first_new, second_new, first_rowmax, first_colmax, second_rowmax, second_colmax,
    own, got, send_l, recv_l, send_m, recv_m, total, recv_l2, send_m2, recv_m2,
    codes, grad, squares, norm_x, norm_y, norm_z, rowmax, colmax, col_y, col_z,
    own_sem, got_sem, code_sem, l_sem, m_sem, l2_sem, m2_sem, small_sem,
    got_send, l_send, m_send, l2_send, m2_send, small_send,
):
    slices, _, _, rows, width = own.shape
    quarter = width // 4
    y, z, c, x = (lax.axis_index(a) for a in (Y, Z, C, X))
    at = (y, z)
    names = (Y, Z)
    other = 1 - c

    def step(v, k):
        return lax.rem(v + k, 4)

    for i, ref in enumerate((first_codes, second_codes)):
        pltpu.make_async_copy(ref, codes.at[i], code_sem.at[i]).start()

    def load(p, _):
        pltpu.make_async_copy(
            grads.at[:, :, c, pl.ds(p * rows, rows), :], own.at[p], own_sem.at[p]
        ).start()
        return _

    lax.fori_loop(0, slices, load, 0)

    barrier = pltpu.get_barrier_semaphore()
    peers = [{C: other}]
    for axis, name in enumerate(names):
        for k in (1, 3):
            peers.append({name: step(at[axis], k)})
    for k in (1, 2, 3):
        peers.append({X: step(x, k)})
    for peer in peers:
        pl.semaphore_signal(barrier, inc=1, device_id=peer, device_id_type=MESH)
    pl.semaphore_wait(barrier, len(peers))

    def give(p, _):
        remote(
            grads.at[:, :, other, pl.ds(p * rows, rows), :], got.at[p],
            got_send, got_sem.at[p], {C: other},
        ).start()
        return _

    lax.fori_loop(0, slices, give, 0)

    def columns(axis, slot):
        return pl.ds((2 * axis + slot) * quarter, quarter)

    def pair(p, axis, index, slot):
        where = (p, index, slice(None)) if axis == 0 else (p, slice(None), index)
        where = (*where, slice(None), columns(axis, slot))
        return own[where].astype(jnp.float32) + got[where].astype(jnp.float32)

    def leaves(p, _):
        landed(own.at[p], own_sem.at[p])
        landed(got.at[p], got_sem.at[p])
        for axis in (0, 1):
            me = at[axis]
            for slot, k in DIRS:
                send_l[p, axis, slot, 0] = pair(p, axis, step(me, 2), slot)
                send_l[p, axis, slot, 1] = pair(p, axis, step(me, k), 1 - slot)
                remote(
                    send_l.at[p, axis, slot], recv_l.at[p, axis, slot],
                    l_send, l_sem.at[p, axis, slot], {names[axis]: step(me, k)},
                ).start()
        return _

    lax.fori_loop(0, slices, leaves, 0)

    def middles(p, _):
        for axis in (0, 1):
            me = at[axis]
            for slot, k in DIRS:
                landed(recv_l.at[p, axis, slot], l_sem.at[p, axis, slot])
                send_m[p, axis, slot] = pair(p, axis, step(me, k), slot) + recv_l[p, axis, slot, 0]
                remote(
                    send_m.at[p, axis, slot], recv_m.at[p, axis, slot],
                    m_send, m_sem.at[p, axis, slot], {names[axis]: step(me, k)},
                ).start()
        return _

    lax.fori_loop(0, slices, middles, 0)

    for i, ref in enumerate((first_codes, second_codes)):
        pltpu.make_async_copy(ref, codes.at[i], code_sem.at[i]).wait()
    for i, (row_ref, col_ref, out, factor) in enumerate((
        (first_rows, first_columns, first_new, beta_first / 7.0),
        (second_rows, second_columns, second_new, beta_second / 15.0),
    )):
        row_count = row_ref.shape[1]
        by_row = jnp.transpose(jnp.broadcast_to(row_ref[...], (128, row_count)))
        for j in range(width // 128):
            cols = pl.ds(j * 128, 128)
            bound = jnp.minimum(by_row, col_ref[:, cols])
            out[:, cols] = codes[i, :, cols].astype(jnp.float32) * factor * bound

    def totals(p, _):
        for axis in (0, 1):
            me, over, across = at[axis], at[1 - axis], names[1 - axis]
            for slot, k in DIRS:
                landed(recv_m.at[p, axis, slot], m_sem.at[p, axis, slot])
                total[p, axis, slot] = (
                    pair(p, axis, me, slot) + recv_m[p, axis, slot] + recv_l[p, axis, 1 - slot, 1]
                )
            for slot, k in DIRS:
                for unit, (which, index) in enumerate(((slot, 2), (1 - slot, k))):
                    remote(
                        total.at[p, axis, which, step(over, index)], recv_l2.at[p, axis, slot, unit],
                        l2_send, l2_sem.at[p, axis, slot], {across: step(over, k)},
                    ).start()
        return _

    lax.fori_loop(0, slices, totals, 0)

    def middles2(p, _):
        for axis in (0, 1):
            over, across = at[1 - axis], names[1 - axis]
            for slot, k in DIRS:
                landed(recv_l2.at[p, axis, slot], l2_sem.at[p, axis, slot])
                send_m2[p, axis, slot] = (
                    total[p, axis, slot, step(over, k)] + recv_l2[p, axis, slot, 0]
                )
                remote(
                    send_m2.at[p, axis, slot], recv_m2.at[p, axis, slot],
                    m2_send, m2_sem.at[p, axis, slot], {across: step(over, k)},
                ).start()
        return _

    lax.fori_loop(0, slices, middles2, 0)

    squares[...] = jnp.zeros_like(squares)

    def finish(p, _):
        for axis in (0, 1):
            over = at[1 - axis]
            for slot, k in DIRS:
                landed(recv_m2.at[p, axis, slot], m2_sem.at[p, axis, slot])
                value = (
                    total[p, axis, slot, over] + recv_m2[p, axis, slot]
                    + recv_l2[p, axis, 1 - slot, 1]
                )
                grad[pl.ds(pl.multiple_of(p * rows, rows), rows), columns(axis, slot)] = value
                sq = value * value
                part = sq[:, :128]
                for j in range(1, quarter // 128):
                    part = part + sq[:, j * 128 : (j + 1) * 128]
                squares[...] += jnp.sum(part.reshape(rows // 8, 8, 128), axis=0)
        return _

    lax.fori_loop(0, slices, finish, 0)

    def exchange(value_ref, slots, targets, sem):
        for i, target in enumerate(targets):
            remote(value_ref, slots.at[i], small_send.at[sem], small_sem.at[sem], target).start()

    x_peers = [{X: step(x, k)} for k in (1, 2, 3)]
    y_peers = [
        {Y: step(y, ky), C: (other if kc else c)}
        for ky in range(4) for kc in range(2) if ky or kc
    ]
    z_peers = [{Z: step(z, k)} for k in (1, 2, 3)]

    for i, (slots, targets) in enumerate(((norm_x, x_peers), (norm_y, y_peers), (norm_z, z_peers))):
        exchange(squares, slots, targets, i)
        landed(slots, small_sem.at[i])
        pltpu.make_async_copy(slots, slots, small_send.at[i]).wait()
        squares[...] += jnp.sum(slots[...], axis=0)

    square_sum = jnp.sum(squares[...], keepdims=True)
    clip_scale = clip_limit / jnp.maximum(jnp.sqrt(square_sum), clip_limit)

    tile = 32
    first_top = jnp.zeros((8, width), jnp.float32)
    second_top = jnp.zeros((8, width), jnp.float32)

    def moment(t, tops):
        here = pl.ds(pl.multiple_of(t * tile, tile), tile)
        clipped = clip_scale * grad[here, :]
        first = first_new[here, :] + (1.0 - beta_first) * clipped
        second = second_new[here, :] + (1.0 - beta_second) * clipped * clipped
        first_new[here, :] = first
        second_new[here, :] = second
        outs = []
        for i, (value, top) in enumerate(((jnp.abs(first), tops[0]), (second, tops[1]))):
            outs.append(jnp.maximum(top, jnp.max(value.reshape(tile // 8, 8, width), axis=0)))
            most = value[:, :128]
            for j in range(1, width // 128):
                most = jnp.maximum(most, value[:, j * 128 : (j + 1) * 128])
            rowmax[i, here, :] = most
        return tuple(outs)

    first_top, second_top = lax.fori_loop(0, grad.shape[0] // tile, moment, (first_top, second_top))
    colmax[0:1, :] = jnp.max(first_top, axis=0, keepdims=True)
    colmax[1:2, :] = jnp.max(second_top, axis=0, keepdims=True)

    exchange(colmax, col_y, y_peers, 3)
    first_row = jnp.max(jnp.transpose(rowmax[0]), axis=0, keepdims=True)
    first_rowmax[...] = jnp.maximum(first_row, scale_floor)
    second_rowmax[...] = jnp.max(jnp.transpose(rowmax[1]), axis=0, keepdims=True)
    landed(col_y, small_sem.at[3])
    pltpu.make_async_copy(col_y, col_y, small_send.at[3]).wait()
    colmax[...] = jnp.maximum(colmax[...], jnp.max(col_y[...], axis=0))
    exchange(colmax, col_z, z_peers, 4)
    landed(col_z, small_sem.at[4])
    result = jnp.maximum(colmax[...], jnp.max(col_z[...], axis=0))
    first_colmax[...] = jnp.maximum(result[0:1], scale_floor)
    second_colmax[...] = result[1:2]
    pltpu.make_async_copy(col_z, col_z, small_send.at[4]).wait()

    landed(got, got_send)
    landed(send_l, l_send)
    landed(send_m, m_send)
    landed(recv_l2, l2_send)
    landed(send_m2, m2_send)


def local(
    grad_parts, first_codes, first_rows, first_columns, second_codes, second_rows, second_columns
):
    layer_count, _, row_count, col_count = grad_parts.shape
    entries = layer_count * lax.axis_size(X) * row_count * col_count
    clip_limit = clip_rms * math.sqrt(entries)
    own_rows = first_codes.shape[1]
    rows = own_rows // SLICES
    q = col_count // 4
    f32, bf16 = jnp.float32, jnp.bfloat16
    shape = jax.ShapeDtypeStruct
    vmem = pltpu.VMEM
    dma = pltpu.SemaphoreType.DMA
    grads = grad_parts.reshape(4, 4, 2, own_rows, col_count)
    any_spec = pl.BlockSpec(memory_space=pl.ANY)
    vmem_spec = pl.BlockSpec(memory_space=pltpu.VMEM)
    n = SLICES
    first_new, second_new, first_rowmax, first_colmax, second_rowmax, second_colmax = pl.pallas_call(
        functools.partial(kernel, clip_limit),
        out_shape=(
            shape((own_rows, col_count), f32), shape((own_rows, col_count), f32),
            shape((1, own_rows), f32), shape((1, col_count), f32),
            shape((1, own_rows), f32), shape((1, col_count), f32),
        ),
        in_specs=[any_spec, any_spec, vmem_spec, vmem_spec, any_spec, vmem_spec, vmem_spec],
        out_specs=[vmem_spec] * 6,
        scratch_shapes=[
            vmem((n, 4, 4, rows, col_count), bf16),
            vmem((n, 4, 4, rows, col_count), bf16),
            vmem((n, 2, 2, 2, 4, rows, q), f32),
            vmem((n, 2, 2, 2, 4, rows, q), f32),
            vmem((n, 2, 2, 4, rows, q), f32),
            vmem((n, 2, 2, 4, rows, q), f32),
            vmem((n, 2, 2, 4, rows, q), f32),
            vmem((n, 2, 2, 2, rows, q), f32),
            vmem((n, 2, 2, rows, q), f32),
            vmem((n, 2, 2, rows, q), f32),
            vmem((2, own_rows, col_count), jnp.int32),
            vmem((own_rows, col_count), f32),
            vmem((8, 128), f32),
            vmem((3, 8, 128), f32),
            vmem((7, 8, 128), f32),
            vmem((3, 8, 128), f32),
            vmem((2, own_rows, 128), f32),
            vmem((2, col_count), f32),
            vmem((7, 2, col_count), f32),
            vmem((3, 2, col_count), f32),
            dma((n,)), dma((n,)), dma((2,)),
            dma((n, 2, 2)), dma((n, 2, 2)), dma((n, 2, 2)), dma((n, 2, 2)), dma((5,)),
            dma, dma, dma, dma, dma, dma((5,)),
        ],
        compiler_params=pltpu.CompilerParams(
            collective_id=0, has_side_effects=True, vmem_limit_bytes=67043328
        ),
        name="clipped_adam",
    )(
        grads, first_codes[0], first_rows, first_columns, second_codes[0], second_rows,
        second_columns,
    )
    direction = first_new / (jnp.sqrt(second_new) + epsilon)
    first_scaled = first_new / jnp.minimum(first_rowmax[0, :, None], first_colmax)
    second_scaled = second_new / jnp.minimum(second_rowmax[0, :, None], second_colmax)
    return (
        direction[None], first_scaled[None], second_scaled[None],
        first_rowmax, first_colmax, second_rowmax, second_colmax,
    )


def solution(mesh):
    torus = Mesh(mesh.devices.reshape(mesh.shape["section"], 4, 4, 2), (X, Y, Z, C))
    placed = (
        P(X, FSDP, None, None),
        P(X, FSDP, None),
        P(X, FSDP),
        P(X, None),
        P(X, FSDP, None),
        P(X, FSDP),
        P(X, None),
    )
    return jax.shard_map(
        local,
        mesh=torus,
        in_specs=placed,
        out_specs=(
            P(X, FSDP, None), P(X, FSDP, None), P(X, FSDP, None),
            P(X, FSDP), P(X, None), P(X, FSDP), P(X, None),
        ),
        check_vma=False,
    )
```

time: 254 us -> 127 us (0.50)
  waiting for transfers between devices: 173 us -> 0 us
  Pallas kernels: 0 us -> 118 us
  blocking collectives: 34.7 us -> 0 us
  local copies, waits for them, and re-layouts: 19.5 us -> 4.97 us
  between operations: 14.9 us -> 0.64 us
  starting transfers between devices: 3.94 us -> 0 us
  other arithmetic: 7.02 us -> 3.81 us
    pallas_call x0 -> x1, Pallas kernels: none -> 118 us  [local(): pl.pallas_call(functools.partial(kernel, clip_limit), out_shape=(shape((o...]
    unnamed x3 -> x0, waiting for transfers between devices: 115 us -> none
    reduce_scatter x1 -> x0, waiting for transfers between devices: 48.8 us -> none  [sum_by_chip(): parts = lax.psum_scatter(parts, core, scatter_dimension=0, tiled=True)]
    psum x4 -> x0, blocking collectives: 34.7 us -> none  [by_axis(): value = lax.psum(value, axis)]
    reshape x1 -> x0, local copies, waits for them, and re-layouts: 18.6 us -> none  [sum_by_chip(): parts = parts.reshape(*sizes, *inside).swapaxes(0, 1).reshape(-1, *inside)]
    all_to_all x1 -> x0, waiting for transfers between devices: 9.05 us -> none  [copy_for_each(): return lax.all_to_all(copies, axis, split_axis=0, concat_axis=0, tiled=True)]
    unnamed x18 -> x4, local copies, waits for them, and re-layouts: 0.06 us -> 4.97 us
    all_to_all x1 -> x0, starting transfers between devices: 3.86 us -> none  [copy_for_each(): return lax.all_to_all(copies, axis, split_axis=0, concat_axis=0, tiled=True)]
  transfers between devices with their start and end apart: 3 -> 0, of which waited for: 3 -> 0; matrix products, arithmetic and copies ran while one was open for 0% -> 0% of each run, Pallas kernels for 0% -> 0%
where the time goes in v1:
time: 127 us
  Pallas kernels  118 us (93%)
  local copies, waits for them, and re-layouts  4.97 us (4%)
  other arithmetic  3.81 us (3%)
    pallas_call x1, Pallas kernels, local(): pl.pallas_call(functools.partial(kernel, clip_limit), out_shape=(shape((o...  118 us
    unnamed x4, local copies, waits for them, and re-layouts  4.97 us
    broadcast_in_dim x1, other arithmetic, local(): second_scaled[None]  3.81 us

profile of v1, /device:TPU:1, one launch (start us, length us, event | category | flops | bytes accessed | tf_op | source)
XLA Modules:
  0.0 127.2 jit_solution(3086086051139722096)
XLA Ops:
  0.6 117.7 %clipped_adam.1 = (f32[256,1024]{1,0:T(8,128)}, f32[256,1024]{1,0:T(8,128)}, f32[1,256]{1,0:T(1,128)}, f32[1,1024]{1,0:T(1,128)}, f32[1,256]{1,0:T(1,128)}, /*index=5*/f32[1,1024]{1,0:T(1,128)}) custom-call(bf16[4,4,2,256,1024]{4,3,2,1,0:T(8,128)(2,1)} %bitcast.13, s32[256,1024]{1,0:T(8,128)} %bitcast.14, f32[1,256]{1,0:T(1,128)} %first_rows.1, ...), custom_call_target="tpu_custom_call" | custom-call | tf_op jit(solution)/shard_map/clipped_adam/pallas_call | solution.py:275
  118.4 3.8 %divide_bitcast_fusion = (f32[1,256,1024]{2,1,0:T(8,128)}, f32[1,256,1024]{2,1,0:T(8,128)}, f32[1,256,1024]{2,1,0:T(8,128)}) fusion(f32[256,1024]{1,0:T(8,128)} %get-tuple-element.14, f32[1024]{0:T(1024)} %bitcast.16, f32[256]{0:T(256)} %bitcast.18, f32[256,1024]{1,0:T(8,128)} %get-tuple-element.13, f32[1024]{0:T(1024)} %bitcast.17, f32[256]{0:T(256)} %bitcast.19), kind=kLoop, calls=%fused_computation | loop fusion | flops 1572864 | bytes 5253120 | tf_op jit(solution)/shard_map/broadcast_in_dim | solution.py:321
  122.2 1.2 copy.18
  123.4 1.3 %copy.19 = f32[1,1024]{1,0:T(1,128)} copy(f32[1,1024]{1,0:T(1,128)} %get-tuple-element.33) | data formatting | bytes 8192
  124.7 1.2 copy.20
  125.9 1.3 copy.21

commit v2 on v1

--- a/solution.py
+++ b/solution.py
@@ -20,6 +20,8 @@
 scale_floor = 0.001
 
 SLICES = 8
+LEVELS = 32766.0
+TINY = 2e-34
 DIRS = ((0, 1), (1, 3))
 
 
@@ -34,14 +36,29 @@
     pltpu.make_async_copy(buf, buf, sem).wait()
 
 
+def put(value, codes, tops, key):
+    top = jnp.maximum(jnp.max(jnp.abs(value), axis=0, keepdims=True), TINY)
+    scaled = jnp.round(value * (LEVELS / top))
+    codes[key] = scaled.astype(jnp.int32).astype(jnp.int16)
+    *lead, row = key
+    tops[(*lead, pl.ds(row, 1))] = top
+
+
+def take(codes, tops, key):
+    *lead, row = key
+    unit = tops[(*lead, pl.ds(row, 1))] * (1.0 / LEVELS)
+    return codes[key].astype(jnp.int32).astype(jnp.float32) * unit
+
+
 def kernel(
     clip_limit,
     grads, first_codes, first_rows, first_columns, second_codes, second_rows, second_columns,
     first_new, second_new, first_rowmax, first_colmax, second_rowmax, second_colmax,
-    own, got, send_l, recv_l, send_m, recv_m, total, recv_l2, send_m2, recv_m2,
+    own, got, sent_l, sent_lt, came_l, came_lt, sent_m, sent_mt, came_m, came_mt, total,
+    sent_l2, sent_l2t, came_l2, came_l2t, sent_m2, sent_m2t, came_m2, came_m2t,
     codes, grad, squares, norm_x, norm_y, norm_z, rowmax, colmax, col_y, col_z,
     own_sem, got_sem, code_sem, l_sem, m_sem, l2_sem, m2_sem, small_sem,
-    got_send, l_send, m_send, l2_send, m2_send, small_send,
+    got_send, sends, small_send,
 ):
     slices, _, _, rows, width = own.shape
     quarter = width // 4
@@ -53,9 +70,6 @@
     def step(v, k):
         return lax.rem(v + k, 4)
 
-    for i, ref in enumerate((first_codes, second_codes)):
-        pltpu.make_async_copy(ref, codes.at[i], code_sem.at[i]).start()
-
     def load(p, _):
         pltpu.make_async_copy(
             grads.at[:, :, c, pl.ds(p * rows, rows), :], own.at[p], own_sem.at[p]
@@ -63,6 +77,8 @@
         return _
 
     lax.fori_loop(0, slices, load, 0)
+    for i, ref in enumerate((first_codes, second_codes)):
+        pltpu.make_async_copy(ref, codes.at[i], code_sem.at[i]).start()
 
     barrier = pltpu.get_barrier_semaphore()
     peers = [{C: other}]
@@ -87,10 +103,18 @@
     def columns(axis, slot):
         return pl.ds((2 * axis + slot) * quarter, quarter)
 
-    def pair(p, axis, index, slot):
-        where = (p, index, slice(None)) if axis == 0 else (p, slice(None), index)
+    def pair(p, axis, index, j, slot):
+        where = (p, index, j) if axis == 0 else (p, j, index)
         where = (*where, slice(None), columns(axis, slot))
         return own[where].astype(jnp.float32) + got[where].astype(jnp.float32)
+
+    def send(kind, key, ref, ref_t, out, out_t, sem, device):
+        remote(ref.at[key], out.at[key], sends.at[kind], sem.at[(*key, 0)], device).start()
+        remote(ref_t.at[key], out_t.at[key], sends.at[kind + 4], sem.at[(*key, 1)], device).start()
+
+    def arrived(key, ref, ref_t, sem):
+        landed(ref.at[key], sem.at[(*key, 0)])
+        landed(ref_t.at[key], sem.at[(*key, 1)])
 
     def leaves(p, _):
         landed(own.at[p], own_sem.at[p])
@@ -98,29 +122,16 @@
         for axis in (0, 1):
             me = at[axis]
             for slot, k in DIRS:
-                send_l[p, axis, slot, 0] = pair(p, axis, step(me, 2), slot)
-                send_l[p, axis, slot, 1] = pair(p, axis, step(me, k), 1 - slot)
-                remote(
-                    send_l.at[p, axis, slot], recv_l.at[p, axis, slot],
-                    l_send, l_sem.at[p, axis, slot], {names[axis]: step(me, k)},
-                ).start()
+                for j in range(4):
+                    value = pair(p, axis, step(me, 2), j, slot)
+                    put(value, sent_l, sent_lt, (p, axis, slot, j))
+                    value = pair(p, axis, step(me, k), j, 1 - slot)
+                    put(value, sent_l, sent_lt, (p, axis, slot, 4 + j))
+                send(0, (p, axis, slot), sent_l, sent_lt, came_l, came_lt, l_sem,
+                     {names[axis]: step(me, k)})
         return _
 
     lax.fori_loop(0, slices, leaves, 0)
-
-    def middles(p, _):
-        for axis in (0, 1):
-            me = at[axis]
-            for slot, k in DIRS:
-                landed(recv_l.at[p, axis, slot], l_sem.at[p, axis, slot])
-                send_m[p, axis, slot] = pair(p, axis, step(me, k), slot) + recv_l[p, axis, slot, 0]
-                remote(
-                    send_m.at[p, axis, slot], recv_m.at[p, axis, slot],
-                    m_send, m_sem.at[p, axis, slot], {names[axis]: step(me, k)},
-                ).start()
-        return _
-
-    lax.fori_loop(0, slices, middles, 0)
 
     for i, ref in enumerate((first_codes, second_codes)):
         pltpu.make_async_copy(ref, codes.at[i], code_sem.at[i]).wait()
@@ -135,20 +146,38 @@
             bound = jnp.minimum(by_row, col_ref[:, cols])
             out[:, cols] = codes[i, :, cols].astype(jnp.float32) * factor * bound
 
+    def middles(p, _):
+        for axis in (0, 1):
+            me = at[axis]
+            for slot, k in DIRS:
+                key = (p, axis, slot)
+                arrived(key, came_l, came_lt, l_sem)
+                for j in range(4):
+                    value = pair(p, axis, step(me, k), j, slot)
+                    value = value + take(came_l, came_lt, (*key, j))
+                    put(value, sent_m, sent_mt, (*key, j))
+                send(1, key, sent_m, sent_mt, came_m, came_mt, m_sem, {names[axis]: step(me, k)})
+        return _
+
+    lax.fori_loop(0, slices, middles, 0)
+
     def totals(p, _):
         for axis in (0, 1):
             me, over, across = at[axis], at[1 - axis], names[1 - axis]
             for slot, k in DIRS:
-                landed(recv_m.at[p, axis, slot], m_sem.at[p, axis, slot])
-                total[p, axis, slot] = (
-                    pair(p, axis, me, slot) + recv_m[p, axis, slot] + recv_l[p, axis, 1 - slot, 1]
-                )
+                arrived((p, axis, slot), came_m, came_mt, m_sem)
+                for j in range(4):
+                    total[p, axis, slot, j] = (
+                        pair(p, axis, me, j, slot)
+                        + take(came_m, came_mt, (p, axis, slot, j))
+                        + take(came_l, came_lt, (p, axis, 1 - slot, 4 + j))
+                    )
             for slot, k in DIRS:
                 for unit, (which, index) in enumerate(((slot, 2), (1 - slot, k))):
-                    remote(
-                        total.at[p, axis, which, step(over, index)], recv_l2.at[p, axis, slot, unit],
-                        l2_send, l2_sem.at[p, axis, slot], {across: step(over, k)},
-                    ).start()
+                    value = total[p, axis, which, step(over, index)]
+                    put(value, sent_l2, sent_l2t, (p, axis, slot, unit))
+                send(2, (p, axis, slot), sent_l2, sent_l2t, came_l2, came_l2t, l2_sem,
+                     {across: step(over, k)})
         return _
 
     lax.fori_loop(0, slices, totals, 0)
@@ -157,14 +186,11 @@
         for axis in (0, 1):
             over, across = at[1 - axis], names[1 - axis]
             for slot, k in DIRS:
-                landed(recv_l2.at[p, axis, slot], l2_sem.at[p, axis, slot])
-                send_m2[p, axis, slot] = (
-                    total[p, axis, slot, step(over, k)] + recv_l2[p, axis, slot, 0]
-                )
-                remote(
-                    send_m2.at[p, axis, slot], recv_m2.at[p, axis, slot],
-                    m2_send, m2_sem.at[p, axis, slot], {across: step(over, k)},
-                ).start()
+                key = (p, axis, slot)
+                arrived(key, came_l2, came_l2t, l2_sem)
+                value = total[p, axis, slot, step(over, k)] + take(came_l2, came_l2t, (*key, 0))
+                put(value, sent_m2, sent_m2t, (*key, 0))
+                send(3, key, sent_m2, sent_m2t, came_m2, came_m2t, m2_sem, {across: step(over, k)})
         return _
 
     lax.fori_loop(0, slices, middles2, 0)
@@ -175,10 +201,11 @@
         for axis in (0, 1):
             over = at[1 - axis]
             for slot, k in DIRS:
-                landed(recv_m2.at[p, axis, slot], m2_sem.at[p, axis, slot])
+                arrived((p, axis, slot), came_m2, came_m2t, m2_sem)
                 value = (
-                    total[p, axis, slot, over] + recv_m2[p, axis, slot]
-                    + recv_l2[p, axis, 1 - slot, 1]
+                    total[p, axis, slot, over]
+                    + take(came_m2, came_m2t, (p, axis, slot, 0))
+                    + take(came_l2, came_l2t, (p, axis, 1 - slot, 1))
                 )
                 grad[pl.ds(pl.multiple_of(p * rows, rows), rows), columns(axis, slot)] = value
                 sq = value * value
@@ -249,10 +276,30 @@
     pltpu.make_async_copy(col_z, col_z, small_send.at[4]).wait()
 
     landed(got, got_send)
-    landed(send_l, l_send)
-    landed(send_m, m_send)
-    landed(recv_l2, l2_send)
-    landed(send_m2, m2_send)
+    for kind, (ref, ref_t) in enumerate((
+        (sent_l, sent_lt), (sent_m, sent_mt), (sent_l2, sent_l2t), (sent_m2, sent_m2t),
+    )):
+        landed(ref, sends.at[kind])
+        landed(ref_t, sends.at[kind + 4])
+
+
+def scale(
+    first_new, second_new, first_rowmax, first_colmax, second_rowmax, second_colmax,
+    direction, first_scaled, second_scaled, *maxima,
+):
+    first, second = first_new[...], second_new[...]
+    direction[...] = first / (jnp.sqrt(second) + epsilon)
+    rows, width = first.shape
+    for value, row, col, out in (
+        (first, first_rowmax, first_colmax, first_scaled),
+        (second, second_rowmax, second_colmax, second_scaled),
+    ):
+        by_row = jnp.transpose(jnp.broadcast_to(row[...], (128, rows)))
+        for j in range(width // 128):
+            cols = slice(j * 128, j * 128 + 128)
+            out[:, cols] = value[:, cols] / jnp.minimum(by_row, col[:, cols])
+    for ref, out in zip((first_rowmax, first_colmax, second_rowmax, second_colmax), maxima):
+        out[...] = ref[...]
 
 
 def local(
@@ -272,6 +319,10 @@
     any_spec = pl.BlockSpec(memory_space=pl.ANY)
     vmem_spec = pl.BlockSpec(memory_space=pltpu.VMEM)
     n = SLICES
+
+    def coded(count):
+        return vmem((n, 2, 2, count, rows, q), jnp.int16), vmem((n, 2, 2, count, q), f32)
+
     first_new, second_new, first_rowmax, first_colmax, second_rowmax, second_colmax = pl.pallas_call(
         functools.partial(kernel, clip_limit),
         out_shape=(
@@ -284,14 +335,11 @@
         scratch_shapes=[
             vmem((n, 4, 4, rows, col_count), bf16),
             vmem((n, 4, 4, rows, col_count), bf16),
-            vmem((n, 2, 2, 2, 4, rows, q), f32),
-            vmem((n, 2, 2, 2, 4, rows, q), f32),
+            *coded(8), *coded(8),
+            *coded(4), *coded(4),
             vmem((n, 2, 2, 4, rows, q), f32),
-            vmem((n, 2, 2, 4, rows, q), f32),
-            vmem((n, 2, 2, 4, rows, q), f32),
-            vmem((n, 2, 2, 2, rows, q), f32),
-            vmem((n, 2, 2, rows, q), f32),
-            vmem((n, 2, 2, rows, q), f32),
+            *coded(2), *coded(2),
+            *coded(1), *coded(1),
             vmem((2, own_rows, col_count), jnp.int32),
             vmem((own_rows, col_count), f32),
             vmem((8, 128), f32),
@@ -303,8 +351,8 @@
             vmem((7, 2, col_count), f32),
             vmem((3, 2, col_count), f32),
             dma((n,)), dma((n,)), dma((2,)),
-            dma((n, 2, 2)), dma((n, 2, 2)), dma((n, 2, 2)), dma((n, 2, 2)), dma((5,)),
-            dma, dma, dma, dma, dma, dma((5,)),
+            *[dma((n, 2, 2, 2))] * 4, dma((5,)),
+            dma, dma((8,)), dma((5,)),
         ],
         compiler_params=pltpu.CompilerParams(
             collective_id=0, has_side_effects=True, vmem_limit_bytes=67043328
@@ -314,13 +362,20 @@
         grads, first_codes[0], first_rows, first_columns, second_codes[0], second_rows,
         second_columns,
     )
-    direction = first_new / (jnp.sqrt(second_new) + epsilon)
-    first_scaled = first_new / jnp.minimum(first_rowmax[0, :, None], first_colmax)
-    second_scaled = second_new / jnp.minimum(second_rowmax[0, :, None], second_colmax)
-    return (
-        direction[None], first_scaled[None], second_scaled[None],
-        first_rowmax, first_colmax, second_rowmax, second_colmax,
-    )
+    part = own_rows // 2
+    tile = pl.BlockSpec((part, col_count), lambda i: (i, 0))
+    row = pl.BlockSpec((1, part), lambda i: (0, i))
+    column = pl.BlockSpec((1, col_count), lambda i: (0, 0))
+    big, by_row, by_col = (shape(s, f32) for s in ((own_rows, col_count), (1, own_rows), (1, col_count)))
+    direction, first_scaled, second_scaled, *maxima = pl.pallas_call(
+        scale,
+        grid=(own_rows // part,),
+        out_shape=(big, big, big, by_row, by_col, by_row, by_col),
+        in_specs=[tile, tile, row, column, row, column],
+        out_specs=[tile, tile, tile, row, column, row, column],
+        name="scale",
+    )(first_new, second_new, first_rowmax, first_colmax, second_rowmax, second_colmax)
+    return direction[None], first_scaled[None], second_scaled[None], *maxima
 
 
 def solution(mesh):

time: 127 us -> 83.9 us (0.66)
  Pallas kernels: 118 us -> 83.1 us
  local copies, waits for them, and re-layouts: 4.97 us -> 0 us
  other arithmetic: 3.81 us -> 0 us
    pallas_call x1, Pallas kernels: 118 us -> 79.8 us  [local(): pl.pallas_call(functools.partial(kernel, clip_limit), out_shape=(shape((o...]
    unnamed x4 -> x0, local copies, waits for them, and re-layouts: 4.97 us -> none
    broadcast_in_dim x1 -> x0, other arithmetic: 3.81 us -> none  [local(): second_scaled[None]]
    pallas_call x0 -> x1, Pallas kernels: none -> 3.23 us  [local(): pl.pallas_call(scale, grid=(own_rows // part,), out_shape=(big, big, big,...]
where the time goes in v2:
time: 83.9 us; the launch traced here: 83.7 us
  Pallas kernels  83.1 us (99%)
    pallas_call x1, Pallas kernels, local(): pl.pallas_call(functools.partial(kernel, clip_limit), out_shape=(shape((o...  79.8 us
    pallas_call x1, Pallas kernels, local(): pl.pallas_call(scale, grid=(own_rows // part,), out_shape=(big, big, big,...  3.23 us

profile of v2, /device:TPU:1, one launch (start us, length us, event | category | flops | bytes accessed | tf_op | source)
XLA Modules:
  0.0 83.7 jit_solution(9732250036048979825)
XLA Ops:
  0.6 79.8 %clipped_adam.1 = (f32[256,1024]{1,0:T(8,128)}, f32[256,1024]{1,0:T(8,128)}, f32[1,256]{1,0:T(1,128)}, f32[1,1024]{1,0:T(1,128)}, f32[1,256]{1,0:T(1,128)}, /*index=5*/f32[1,1024]{1,0:T(1,128)}) custom-call(bf16[4,4,2,256,1024]{4,3,2,1,0:T(8,128)(2,1)} %bitcast.6, s32[256,1024]{1,0:T(8,128)} %bitcast.7, f32[1,256]{1,0:T(1,128)} %first_rows.1, ...), custom_call_target="tpu_custom_call" | custom-call | tf_op jit(solution)/shard_map/clipped_adam/pallas_call | solution.py:326
  80.5 3.2 %scale.1 = (f32[256,1024]{1,0:T(8,128)}, f32[256,1024]{1,0:T(8,128)}, f32[256,1024]{1,0:T(8,128)}, f32[1,256]{1,0:T(1,128)}, f32[1,1024]{1,0:T(1,128)}, /*index=5*/f32[1,256]{1,0:T(1,128)}, f32[1,1024]{1,0:T(1,128)}) custom-call(f32[256,1024]{1,0:T(8,128)} %get-tuple-element.20.first_new, f32[256,1024]{1,0:T(8,128)} %get-tuple-element.21.second_new, ...), custom_call_target="tpu_custom_call" | custom-call | tf_op jit(solution)/shard_map/scale/pallas_call | solution.py:370

commit v3 on v2

v3 whole, which is shorter than its diff:
```python
import functools
import math

import jax
import jax.numpy as jnp
from jax import lax
from jax.experimental import pallas as pl
from jax.experimental.pallas import tpu as pltpu
from jax.sharding import Mesh
from jax.sharding import PartitionSpec as P

Y, Z, C, X = "fsdp_0", "fsdp_1", "fsdp_2", "section"
FSDP = (Y, Z, C)
MESH = pl.DeviceIdType.MESH

beta_first = 0.9
beta_second = 0.999
clip_rms = 3.0
epsilon = 1e-08
scale_floor = 0.001

SLICES = 8
AHEAD = 3
TILES = 8
LEVELS = 32766.0
TINY = 2e-34
DIRS = ((0, 1), (1, 3))


def remote(src, dst, send, recv, device):
    return pltpu.make_async_remote_copy(
        src_ref=src, dst_ref=dst, send_sem=send, recv_sem=recv,
        device_id=device, device_id_type=MESH,
    )


def landed(buf, sem):
    pltpu.make_async_copy(buf, buf, sem).wait()


def put(values, codes, tops, key):
    rows = []
    for i, value in enumerate(values):
        top = jnp.maximum(jnp.max(jnp.abs(value), axis=0, keepdims=True), TINY) * 1.008
        top = top.astype(jnp.bfloat16).astype(jnp.float32)
        scaled = jnp.round(value * (LEVELS / top))
        codes[(*key, i)] = scaled.astype(jnp.int32).astype(jnp.int16)
        rows.append(top)
    tops[key] = jnp.concatenate(rows, axis=0).astype(tops.dtype)


def take(codes, tops, key, i):
    unit = tops[key].astype(jnp.float32)[i : i + 1] * (1.0 / LEVELS)
    return codes[(*key, i)].astype(jnp.int32).astype(jnp.float32) * unit


def kernel(
    clip_limit,
    grads, first_codes, first_rows, first_columns, second_codes, second_rows, second_columns,
    first_new, second_new, first_rowmax, first_colmax, second_rowmax, second_colmax,
    own, got, sent_l, sent_lt, came_l, came_lt, sent_m, sent_mt, came_m, came_mt, total,
    sent_l2, sent_l2t, came_l2, came_l2t, sent_m2, sent_m2t, came_m2, came_m2t,
    codes, grad, sums, squares, norm_x, norm_p, rowmax, colmax, col_y, col_z,
    first_r, first_c, second_r, second_c, words_ref, gift,
    own_sem, got_sem, code_sem, l_sem, m_sem, l2_sem, m2_sem, small_sem,
    got_send, sends, small_send,
):
    slices, _, _, rows, width = own.shape
    quarter = width // 4
    y, z, c, x = (lax.axis_index(a) for a in (Y, Z, C, X))
    at = (y, z)
    names = (Y, Z)
    other = 1 - c

    def step(v, k):
        return lax.rem(v + k, 4)

    half = pltpu.make_async_copy(grads.at[:, :, other, pl.ds(0, rows), :], gift, own_sem.at[2])
    half.start()

    def load(p, sem):
        pltpu.make_async_copy(
            grads.at[:, :, c, pl.ds(p * rows, rows), :], own.at[p], own_sem.at[sem]
        ).start()
        return sem

    load(0, 0)
    lax.fori_loop(1, slices, load, 1)
    small = (
        (first_rows, first_r), (first_columns, first_c), (second_rows, second_r),
        (second_columns, second_c),
    )
    for i, (ref, to) in enumerate((
        (first_codes, codes.at[0]), (second_codes, codes.at[1]), *small,
    )):
        pltpu.make_async_copy(ref, to, code_sem.at[0 if i < 2 else 1]).start()

    barrier = pltpu.get_barrier_semaphore()
    peers = [{C: other}]
    for axis, name in enumerate(names):
        for k in (1, 3):
            peers.append({name: step(at[axis], k)})
    for k in (1, 2, 3):
        peers.append({X: step(x, k)})
    for peer in peers:
        pl.semaphore_signal(barrier, inc=1, device_id=peer, device_id_type=MESH)
    pl.semaphore_wait(barrier, len(peers))

    def give(p, _):
        remote(
            grads.at[:, :, other, pl.ds(p * rows, rows), :], got.at[p],
            got_send, got_sem.at[p], {C: other},
        ).start()
        return _

    halves = [pl.ds(0, 2 * quarter), pl.ds(2 * quarter, 2 * quarter)]
    half.wait()
    for axis in (0, 1):
        remote(
            gift.at[:, :, :, halves[axis]], got.at[0, :, :, :, halves[axis]],
            got_send, got_sem.at[axis * slices], {C: other},
        ).start()
    lax.fori_loop(1, AHEAD + 1, give, 0)

    def columns(axis, slot):
        return pl.ds((2 * axis + slot) * quarter, quarter)

    def pair(p, axis, index, j, slot):
        where = (p, index, j) if axis == 0 else (p, j, index)
        where = (*where, slice(None), columns(axis, slot))
        return own[where].astype(jnp.float32) + got[where].astype(jnp.float32)

    def send(kind, key, ref, ref_t, out, out_t, sem, device):
        remote(ref.at[key], out.at[key], sends.at[kind], sem, device).start()
        remote(ref_t.at[key], out_t.at[key], sends.at[kind + 4], sem, device).start()

    def arrived(messages, slabs, sem):
        words = messages * (slabs * rows * quarter // 2 + max(slabs, 2) * quarter // 2)
        landed(words_ref.at[:, pl.ds(0, words)], sem)

    def leaves(p, ready):
        @pl.when(p + AHEAD + 1 < slices)
        def _next():
            give(p + AHEAD + 1, 0)

        for axis in (0, 1):
            me = at[axis]
            ready(axis)
            for slot, k in DIRS:
                values = [pair(p, axis, step(me, 2), j, slot) for j in range(4)]
                values += [pair(p, axis, step(me, k), j, 1 - slot) for j in range(4)]
                put(values, sent_l, sent_lt, (p, axis, slot))
                send(0, (p, axis, slot), sent_l, sent_lt, came_l, came_lt, l_sem.at[p],
                     {names[axis]: step(me, k)})

    def first_ready(axis):
        if axis == 0:
            landed(own.at[0], own_sem.at[0])
        landed(got.at[0, :, :, :, halves[axis]], got_sem.at[axis * slices])

    def later(p, _):
        leaves(p, lambda axis: None if axis else landed(got.at[p], got_sem.at[p]))
        return _

    leaves(0, first_ready)
    landed(own.at[pl.ds(1, slices - 1)], own_sem.at[1])
    lax.fori_loop(1, AHEAD, later, 0)

    def middles(p, _):
        arrived(4, 8, l_sem.at[p])
        for axis in (0, 1):
            me = at[axis]
            for slot, k in DIRS:
                key = (p, axis, slot)
                values = [
                    pair(p, axis, step(me, k), j, slot) + take(came_l, came_lt, key, j)
                    for j in range(4)
                ]
                put(values, sent_m, sent_mt, key)
                send(1, key, sent_m, sent_mt, came_m, came_mt, m_sem.at[p],
                     {names[axis]: step(me, k)})
        return _

    def both(p, _):
        @pl.when(p + AHEAD < slices)
        def _next():
            later(p + AHEAD, 0)

        return middles(p, _)

    lax.fori_loop(0, slices, both, 0)

    landed(codes, code_sem.at[0])
    landed(words_ref.at[:, pl.ds(0, 2 * (grad.shape[0] + width))], code_sem.at[1])
    for i, (row_ref, col_ref, out, factor) in enumerate((
        (first_r, first_c, first_new, beta_first / 7.0),
        (second_r, second_c, second_new, beta_second / 15.0),
    )):
        row_count = row_ref.shape[1]
        by_row = jnp.transpose(jnp.broadcast_to(row_ref[...], (128, row_count)))
        for j in range(width // 128):
            cols = pl.ds(j * 128, 128)
            bound = jnp.minimum(by_row, col_ref[:, cols])
            out[:, cols] = codes[i, :, cols].astype(jnp.float32) * factor * bound

    def totals(p, _):
        arrived(4, 4, m_sem.at[p])
        for axis in (0, 1):
            me, over, across = at[axis], at[1 - axis], names[1 - axis]
            for slot, k in DIRS:
                for j in range(4):
                    total[p, axis, slot, j] = (
                        pair(p, axis, me, j, slot)
                        + take(came_m, came_mt, (p, axis, slot), j)
                        + take(came_l, came_lt, (p, axis, 1 - slot), 4 + j)
                    )
            for slot, k in DIRS:
                values = [
                    total[p, axis, which, step(over, index)]
                    for which, index in ((slot, 2), (1 - slot, k))
                ]
                put(values, sent_l2, sent_l2t, (p, axis, slot))
                send(2, (p, axis, slot), sent_l2, sent_l2t, came_l2, came_l2t, l2_sem.at[p],
                     {across: step(over, k)})
        return _

    lax.fori_loop(0, slices, totals, 0)

    def middles2(p, _):
        arrived(4, 2, l2_sem.at[p])
        for axis in (0, 1):
            over, across = at[1 - axis], names[1 - axis]
            for slot, k in DIRS:
                key = (p, axis, slot)
                value = total[p, axis, slot, step(over, k)] + take(came_l2, came_l2t, key, 0)
                put([value], sent_m2, sent_m2t, key)
                send(3, key, sent_m2, sent_m2t, came_m2, came_m2t, m2_sem.at[p],
                     {across: step(over, k)})
        return _

    lax.fori_loop(0, slices, middles2, 0)

    sums[...] = jnp.zeros_like(sums)

    def finish(p, _):
        arrived(4, 1, m2_sem.at[p])
        for axis in (0, 1):
            over = at[1 - axis]
            for slot, k in DIRS:
                value = (
                    total[p, axis, slot, over]
                    + take(came_m2, came_m2t, (p, axis, slot), 0)
                    + take(came_l2, came_l2t, (p, axis, 1 - slot), 1)
                )
                grad[pl.ds(pl.multiple_of(p * rows, rows), rows), columns(axis, slot)] = value
                sq = value * value
                part = sq[:, :128]
                for j in range(1, quarter // 128):
                    part = part + sq[:, j * 128 : (j + 1) * 128]
                sums[...] += jnp.sum(part.reshape(rows // 8, 8, 128), axis=0)
        return _

    lax.fori_loop(0, slices, finish, 0)
    squares[...] = jnp.sum(sums[...], axis=0, keepdims=True)

    def exchange(value_ref, slots, targets, sem):
        for i, target in enumerate(targets):
            remote(value_ref, slots.at[i], small_send.at[sem], small_sem.at[sem], target).start()

    x_peers = [{X: step(x, k)} for k in (1, 2, 3)]
    y_peers = [
        {Y: step(y, ky), C: (other if kc else c)}
        for ky in range(4) for kc in range(2) if ky or kc
    ]
    z_peers = [{Z: step(z, k)} for k in (1, 2, 3)]
    all_peers = [
        {Y: step(y, ky), Z: step(z, kz), C: (other if kc else c)}
        for ky in range(4) for kz in range(4) for kc in range(2) if ky or kz or kc
    ]

    for i, (slots, targets) in enumerate(((norm_x, x_peers), (norm_p, all_peers))):
        exchange(squares, slots, targets, i)
        landed(slots, small_sem.at[i])
        pltpu.make_async_copy(slots, slots, small_send.at[i]).wait()
        squares[...] += jnp.sum(slots[...], axis=0)

    square_sum = jnp.sum(squares[...], keepdims=True)
    clip_scale = clip_limit / jnp.maximum(jnp.sqrt(square_sum), clip_limit)

    tile = 32
    first_top = jnp.zeros((8, width), jnp.float32)
    second_top = jnp.zeros((8, width), jnp.float32)

    def moment(t, tops):
        here = pl.ds(pl.multiple_of(t * tile, tile), tile)
        clipped = clip_scale * grad[here, :]
        first = first_new[here, :] + (1.0 - beta_first) * clipped
        second = second_new[here, :] + (1.0 - beta_second) * clipped * clipped
        first_new[here, :] = first
        second_new[here, :] = second
        outs = []
        for i, (value, top) in enumerate(((jnp.abs(first), tops[0]), (second, tops[1]))):
            outs.append(jnp.maximum(top, jnp.max(value.reshape(tile // 8, 8, width), axis=0)))
            most = value[:, :128]
            for j in range(1, width // 128):
                most = jnp.maximum(most, value[:, j * 128 : (j + 1) * 128])
            rowmax[i, here, :] = most
        return tuple(outs)

    first_top, second_top = lax.fori_loop(0, grad.shape[0] // tile, moment, (first_top, second_top))
    colmax[0:1, :] = jnp.max(first_top, axis=0, keepdims=True)
    colmax[1:2, :] = jnp.max(second_top, axis=0, keepdims=True)

    exchange(colmax, col_y, y_peers, 2)
    first_row = jnp.max(jnp.transpose(rowmax[0]), axis=0, keepdims=True)
    first_rowmax[...] = jnp.maximum(first_row, scale_floor)
    second_rowmax[...] = jnp.max(jnp.transpose(rowmax[1]), axis=0, keepdims=True)

    landed(col_y, small_sem.at[2])
    pltpu.make_async_copy(col_y, col_y, small_send.at[2]).wait()
    colmax[...] = jnp.maximum(colmax[...], jnp.max(col_y[...], axis=0))
    exchange(colmax, col_z, z_peers, 3)
    landed(col_z, small_sem.at[3])
    result = jnp.maximum(colmax[...], jnp.max(col_z[...], axis=0))
    first_colmax[...] = jnp.maximum(result[0:1], scale_floor)
    second_colmax[...] = result[1:2]
    pltpu.make_async_copy(col_z, col_z, small_send.at[3]).wait()

    landed(got, got_send)
    for kind, (ref, ref_t) in enumerate((
        (sent_l, sent_lt), (sent_m, sent_mt), (sent_l2, sent_l2t), (sent_m2, sent_m2t),
    )):
        landed(ref, sends.at[kind])
        landed(ref_t, sends.at[kind + 4])


def scale(
    first_new, second_new, first_rowmax, first_colmax, second_rowmax, second_colmax,
    direction, first_scaled, second_scaled,
    first_row_out, first_col_out, second_row_out, second_col_out,
    out, out_sem, max_sem,
):
    copies = [
        pltpu.make_async_copy(ref, to, max_sem.at[i]) for i, (ref, to) in enumerate((
            (first_rowmax, first_row_out), (first_colmax, first_col_out),
            (second_rowmax, second_row_out), (second_colmax, second_col_out),
        ))
    ]
    for copy in copies:
        copy.start()
    rows, width = first_new.shape
    tile = rows // TILES
    by_row = [
        jnp.transpose(jnp.broadcast_to(ref[...], (128, rows)))
        for ref in (first_rowmax, second_rowmax)
    ]
    for t in range(TILES):
        here = slice(t * tile, (t + 1) * tile)
        for j in range(width // 128):
            cols = slice(j * 128, j * 128 + 128)
            first, second = first_new[here, cols], second_new[here, cols]
            out[0, here, cols] = first / (jnp.sqrt(second) + epsilon)
            out[1, here, cols] = first / jnp.minimum(by_row[0][here], first_colmax[:, cols])
            out[2, here, cols] = second / jnp.minimum(by_row[1][here], second_colmax[:, cols])
        for i, to in enumerate((direction, first_scaled, second_scaled)):
            copy = pltpu.make_async_copy(out.at[i, here], to.at[here], out_sem.at[t, i])
            copy.start()
            copies.append(copy)
    for copy in copies:
        copy.wait()


def local(
    grad_parts, first_codes, first_rows, first_columns, second_codes, second_rows, second_columns
):
    layer_count, _, row_count, col_count = grad_parts.shape
    entries = layer_count * lax.axis_size(X) * row_count * col_count
    clip_limit = clip_rms * math.sqrt(entries)
    own_rows = first_codes.shape[1]
    rows = own_rows // SLICES
    q = col_count // 4
    f32, bf16 = jnp.float32, jnp.bfloat16
    shape = jax.ShapeDtypeStruct
    vmem = pltpu.VMEM
    dma = pltpu.SemaphoreType.DMA
    grads = grad_parts.reshape(4, 4, 2, own_rows, col_count)
    hbm_spec = pl.BlockSpec(memory_space=pltpu.HBM)
    vmem_spec = pl.BlockSpec(memory_space=pltpu.VMEM)
    n = SLICES

    def coded(count):
        return vmem((n, 2, 2, count, rows, q), jnp.int16), vmem((n, 2, 2, count, q), bf16 if count > 1 else f32)

    first_new, second_new, first_rowmax, first_colmax, second_rowmax, second_colmax = pl.pallas_call(
        functools.partial(kernel, clip_limit),
        out_shape=(
            shape((own_rows, col_count), f32), shape((own_rows, col_count), f32),
            shape((1, own_rows), f32), shape((1, col_count), f32),
            shape((1, own_rows), f32), shape((1, col_count), f32),
        ),
        in_specs=[hbm_spec] * 7,
        out_specs=[vmem_spec] * 6,
        scratch_shapes=[
            vmem((n, 4, 4, rows, col_count), bf16),
            vmem((n, 4, 4, rows, col_count), bf16),
            *coded(8), *coded(8),
            *coded(4), *coded(4),
            vmem((n, 2, 2, 4, rows, q), f32),
            *coded(2), *coded(2),
            *coded(1), *coded(1),
            vmem((2, own_rows, col_count), jnp.int32),
            vmem((own_rows, col_count), f32),
            vmem((8, 128), f32),
            vmem((1, 128), f32),
            vmem((3, 1, 128), f32),
            vmem((31, 1, 128), f32),
            vmem((2, own_rows, 128), f32),
            vmem((2, col_count), f32),
            vmem((7, 2, col_count), f32),
            vmem((3, 2, col_count), f32),
            *[vmem((1, own_rows), f32), vmem((1, col_count), f32)] * 2,
            vmem((1, 16 * (rows + 1) * q), f32),
            vmem((4, 4, rows, col_count), bf16),
            dma((3,)), dma((n + 1,)), dma((2,)),
            dma((n,)), dma((n,)), dma((n,)), dma((n,)), dma((4,)),
            dma, dma((8,)), dma((4,)),
        ],
        compiler_params=pltpu.CompilerParams(
            collective_id=0, has_side_effects=True, vmem_limit_bytes=46 * 2**20
        ),
        name="clipped_adam",
    )(
        *(
            pltpu.with_memory_space_constraint(v, pltpu.HBM)
            for v in (
                grads, first_codes[0], first_rows, first_columns, second_codes[0], second_rows,
                second_columns,
            )
        )
    )
    big, by_row, by_col = (shape(s, f32) for s in ((own_rows, col_count), (1, own_rows), (1, col_count)))
    direction, first_scaled, second_scaled, *maxima = pl.pallas_call(
        scale,
        out_shape=(big, big, big, by_row, by_col, by_row, by_col),
        in_specs=[vmem_spec] * 6,
        out_specs=[hbm_spec] * 7,
        scratch_shapes=[vmem((3, own_rows, col_count), f32), dma((TILES, 3)), dma((4,))],
        compiler_params=pltpu.CompilerParams(vmem_limit_bytes=12 * 2**20),
        name="scale",
    )(first_new, second_new, first_rowmax, first_colmax, second_rowmax, second_colmax)
    return direction[None], first_scaled[None], second_scaled[None], *maxima


def solution(mesh):
    torus = Mesh(mesh.devices.reshape(mesh.shape["section"], 4, 4, 2), (X, Y, Z, C))
    placed = (
        P(X, FSDP, None, None),
        P(X, FSDP, None),
        P(X, FSDP),
        P(X, None),
        P(X, FSDP, None),
        P(X, FSDP),
        P(X, None),
    )
    return jax.shard_map(
        local,
        mesh=torus,
        in_specs=placed,
        out_specs=(
            P(X, FSDP, None), P(X, FSDP, None), P(X, FSDP, None),
            P(X, FSDP), P(X, None), P(X, FSDP), P(X, None),
        ),
        check_vma=False,
    )
```

time: 83.9 us -> 74.9 us (0.89)
  Pallas kernels: 83.1 us -> 74.1 us
    pallas_call x1, Pallas kernels: 79.8 us -> 72.1 us  [local(): pl.pallas_call(functools.partial(kernel, clip_limit), out_shape=(shape((o...]
    pallas_call x1, Pallas kernels: 3.23 us -> 2.02 us  [local(): pl.pallas_call(scale, out_shape=(big, big, big, by_row, by_col, by_row, b...]
where the time goes in v3:
time: 74.9 us; the launch traced here: 74.8 us
  Pallas kernels  74.1 us (99%)
    pallas_call x1, Pallas kernels, local(): pl.pallas_call(functools.partial(kernel, clip_limit), out_shape=(shape((o...  72.1 us
    pallas_call x1, Pallas kernels, local(): pl.pallas_call(scale, out_shape=(big, big, big, by_row, by_col, by_row, b...  2.02 us

profile of v3, /device:TPU:1, one launch (start us, length us, event | category | flops | bytes accessed | tf_op | source)
XLA Modules:
  0.0 74.8 jit_solution(13844804840108212856)
XLA Ops:
  0.6 72.1 %clipped_adam.1 = (f32[256,1024]{1,0:T(8,128)S(1)}, f32[256,1024]{1,0:T(8,128)S(1)}, f32[1,256]{1,0:T(1,128)S(1)}, f32[1,1024]{1,0:T(1,128)S(1)}, f32[1,256]{1,0:T(1,128)S(1)}, /*index=5*/f32[1,1024]{1,0:T(1,128)S(1)}) custom-call(bf16[4,4,2,256,1024]{4,3,2,1,0:T(8,128)(2,1)} %bitcast.6, s32[256,1024]{1,0:T(8,128)} %bitcast.7, f32[1,256]{1,0:T(1,128)} %first_rows.1, ...), custom_call_target="tpu_custom_call" | custom-call | tf_op jit(solution)/shard_map/clipped_adam/pallas_call | solution.py:394
  72.7 2.0 %scale.1 = (f32[256,1024]{1,0:T(8,128)}, f32[256,1024]{1,0:T(8,128)}, f32[256,1024]{1,0:T(8,128)}, f32[1,256]{1,0:T(1,128)}, f32[1,1024]{1,0:T(1,128)}, /*index=5*/f32[1,256]{1,0:T(1,128)}, f32[1,1024]{1,0:T(1,128)}) custom-call(f32[256,1024]{1,0:T(8,128)S(1)} %get-tuple-element.20.first_new, f32[256,1024]{1,0:T(8,128)S(1)} %get-tuple-element.21.second_new, ...), custom_call_target="tpu_custom_call" | custom-call | tf_op jit(solution)/shard_map/scale/pallas_call | solution.py:442

commit v4 on v3

--- a/solution.py
+++ b/solution.py
@@ -21,6 +21,7 @@
 
 SLICES = 8
 AHEAD = 3
+ROUNDS = 6
 TILES = 8
 LEVELS = 32766.0
 TINY = 2e-34
@@ -60,10 +61,10 @@
     first_new, second_new, first_rowmax, first_colmax, second_rowmax, second_colmax,
     own, got, sent_l, sent_lt, came_l, came_lt, sent_m, sent_mt, came_m, came_mt, total,
     sent_l2, sent_l2t, came_l2, came_l2t, sent_m2, sent_m2t, came_m2, came_m2t,
-    codes, grad, sums, squares, norm_x, norm_p, rowmax, colmax, col_y, col_z,
+    codes, grad, sums, squares, norm_c, norm_p, rowmax, colmax, col_c, col_z,
     first_r, first_c, second_r, second_c, words_ref, gift,
     own_sem, got_sem, code_sem, l_sem, m_sem, l2_sem, m2_sem, small_sem,
-    got_send, sends, small_send,
+    got_send, sends, small_send, word_sem,
 ):
     slices, _, _, rows, width = own.shape
     quarter = width // 4
@@ -74,6 +75,16 @@
 
     def step(v, k):
         return lax.rem(v + k, 4)
+
+    barrier = pltpu.get_barrier_semaphore()
+    peers = [{C: other}]
+    for axis, name in enumerate(names):
+        for k in (1, 3):
+            peers.append({name: step(at[axis], k)})
+    for k in (1, 3):
+        peers.append({X: step(x, k)})
+    for peer in peers:
+        pl.semaphore_signal(barrier, inc=1, device_id=peer, device_id_type=MESH)
 
     half = pltpu.make_async_copy(grads.at[:, :, other, pl.ds(0, rows), :], gift, own_sem.at[2])
     half.start()
@@ -95,16 +106,18 @@
     )):
         pltpu.make_async_copy(ref, to, code_sem.at[0 if i < 2 else 1]).start()
 
-    barrier = pltpu.get_barrier_semaphore()
-    peers = [{C: other}]
-    for axis, name in enumerate(names):
-        for k in (1, 3):
-            peers.append({name: step(at[axis], k)})
-    for k in (1, 2, 3):
-        peers.append({X: step(x, k)})
-    for peer in peers:
-        pl.semaphore_signal(barrier, inc=1, device_id=peer, device_id_type=MESH)
     pl.semaphore_wait(barrier, len(peers))
+    def spread_word(p):
+        @pl.when((p > 0) & (p <= ROUNDS))
+        def _hear():
+            pl.semaphore_wait(word_sem.at[p - 1], len(peers))
+
+        @pl.when(p < ROUNDS)
+        def _tell():
+            for peer in peers:
+                pl.semaphore_signal(
+                    word_sem.at[p], inc=1, device_id=peer, device_id_type=MESH
+                )
 
     def give(p, _):
         remote(
@@ -182,6 +195,8 @@
         return _
 
     def both(p, _):
+        spread_word(p)
+
         @pl.when(p + AHEAD < slices)
         def _next():
             later(p + AHEAD, 0)
@@ -267,24 +282,38 @@
         for i, target in enumerate(targets):
             remote(value_ref, slots.at[i], small_send.at[sem], small_sem.at[sem], target).start()
 
-    x_peers = [{X: step(x, k)} for k in (1, 2, 3)]
-    y_peers = [
-        {Y: step(y, ky), C: (other if kc else c)}
-        for ky in range(4) for kc in range(2) if ky or kc
-    ]
-    z_peers = [{Z: step(z, k)} for k in (1, 2, 3)]
-    all_peers = [
-        {Y: step(y, ky), Z: step(z, kz), C: (other if kc else c)}
-        for ky in range(4) for kz in range(4) for kc in range(2) if ky or kz or kc
-    ]
-
-    for i, (slots, targets) in enumerate(((norm_x, x_peers), (norm_p, all_peers))):
-        exchange(squares, slots, targets, i)
-        landed(slots, small_sem.at[i])
-        pltpu.make_async_copy(slots, slots, small_send.at[i]).wait()
-        squares[...] += jnp.sum(slots[...], axis=0)
-
-    square_sum = jnp.sum(squares[...], keepdims=True)
+    def spread(value_ref, slots, places, sem):
+        @pl.when(c == 1)
+        def _send():
+            for i, place in enumerate(places):
+                for core in range(2):
+                    remote(
+                        value_ref, slots.at[i], small_send.at[sem], small_sem.at[sem],
+                        {**place, C: core},
+                    ).start()
+
+        landed(slots, small_sem.at[sem])
+
+    def spread_done(slots, sem):
+        @pl.when(c == 1)
+        def _left():
+            landed(slots, small_send.at[sem])
+            landed(slots, small_send.at[sem])
+
+    hops = (0, 1, 2, 1)
+
+    def far_first(at_x):
+        places = [(kx, ky, kz) for kx in at_x for ky in range(4) for kz in range(4)]
+        places = [place for place in places if any(place)]
+        places.sort(key=lambda place: -sum(hops[k] for k in place))
+        return [{X: step(x, kx), Y: step(y, ky), Z: step(z, kz)} for kx, ky, kz in places]
+
+    exchange(squares, norm_c, [{C: other}], 0)
+    landed(norm_c, small_sem.at[0])
+    landed(norm_c, small_send.at[0])
+    squares[...] += norm_c[0]
+    spread(squares, norm_p, far_first(range(4)), 1)
+    square_sum = jnp.sum(squares[...] + jnp.sum(norm_p[...], axis=0), keepdims=True)
     clip_scale = clip_limit / jnp.maximum(jnp.sqrt(square_sum), clip_limit)
 
     tile = 32
@@ -311,20 +340,20 @@
     colmax[0:1, :] = jnp.max(first_top, axis=0, keepdims=True)
     colmax[1:2, :] = jnp.max(second_top, axis=0, keepdims=True)
 
-    exchange(colmax, col_y, y_peers, 2)
+    exchange(colmax, col_c, [{C: other}], 2)
     first_row = jnp.max(jnp.transpose(rowmax[0]), axis=0, keepdims=True)
     first_rowmax[...] = jnp.maximum(first_row, scale_floor)
     second_rowmax[...] = jnp.max(jnp.transpose(rowmax[1]), axis=0, keepdims=True)
 
-    landed(col_y, small_sem.at[2])
-    pltpu.make_async_copy(col_y, col_y, small_send.at[2]).wait()
-    colmax[...] = jnp.maximum(colmax[...], jnp.max(col_y[...], axis=0))
-    exchange(colmax, col_z, z_peers, 3)
-    landed(col_z, small_sem.at[3])
+    landed(col_c, small_sem.at[2])
+    landed(col_c, small_send.at[2])
+    colmax[...] = jnp.maximum(colmax[...], col_c[0])
+    spread(colmax, col_z, far_first((0,)), 3)
     result = jnp.maximum(colmax[...], jnp.max(col_z[...], axis=0))
     first_colmax[...] = jnp.maximum(result[0:1], scale_floor)
     second_colmax[...] = result[1:2]
-    pltpu.make_async_copy(col_z, col_z, small_send.at[3]).wait()
+    spread_done(norm_p, 1)
+    spread_done(col_z, 3)
 
     landed(got, got_send)
     for kind, (ref, ref_t) in enumerate((
@@ -412,18 +441,18 @@
             vmem((own_rows, col_count), f32),
             vmem((8, 128), f32),
             vmem((1, 128), f32),
-            vmem((3, 1, 128), f32),
-            vmem((31, 1, 128), f32),
+            vmem((1, 1, 128), f32),
+            vmem((63, 1, 128), f32),
             vmem((2, own_rows, 128), f32),
             vmem((2, col_count), f32),
-            vmem((7, 2, col_count), f32),
-            vmem((3, 2, col_count), f32),
+            vmem((1, 2, col_count), f32),
+            vmem((15, 2, col_count), f32),
             *[vmem((1, own_rows), f32), vmem((1, col_count), f32)] * 2,
             vmem((1, 16 * (rows + 1) * q), f32),
             vmem((4, 4, rows, col_count), bf16),
             dma((3,)), dma((n + 1,)), dma((2,)),
             dma((n,)), dma((n,)), dma((n,)), dma((n,)), dma((4,)),
-            dma, dma((8,)), dma((4,)),
+            dma, dma((8,)), dma((4,)), pltpu.SemaphoreType.REGULAR((ROUNDS,)),
         ],
         compiler_params=pltpu.CompilerParams(
             collective_id=0, has_side_effects=True, vmem_limit_bytes=46 * 2**20

time: 74.9 us -> 72.4 us (0.967)
  Pallas kernels: 74.1 us -> 71.7 us
    pallas_call x1, Pallas kernels: 72.1 us -> 69.7 us  [local(): pl.pallas_call(functools.partial(kernel, clip_limit), out_shape=(shape((o...]
where the time goes in v4:
time: 72.4 us; the launch traced here: 72.3 us
  Pallas kernels  71.7 us (99%)
    pallas_call x1, Pallas kernels, local(): pl.pallas_call(functools.partial(kernel, clip_limit), out_shape=(shape((o...  69.7 us
    pallas_call x1, Pallas kernels, local(): pl.pallas_call(scale, out_shape=(big, big, big, by_row, by_col, by_row, b...  2.02 us

profile of v4, /device:TPU:1, one launch (start us, length us, event | category | flops | bytes accessed | tf_op | source)
XLA Modules:
  0.0 72.3 jit_solution(10077561423513850651)
XLA Ops:
  0.6 69.7 %clipped_adam.1 = (f32[256,1024]{1,0:T(8,128)S(1)}, f32[256,1024]{1,0:T(8,128)S(1)}, f32[1,256]{1,0:T(1,128)S(1)}, f32[1,1024]{1,0:T(1,128)S(1)}, f32[1,256]{1,0:T(1,128)S(1)}, /*index=5*/f32[1,1024]{1,0:T(1,128)S(1)}) custom-call(bf16[4,4,2,256,1024]{4,3,2,1,0:T(8,128)(2,1)} %bitcast.6, s32[256,1024]{1,0:T(8,128)} %bitcast.7, f32[1,256]{1,0:T(1,128)} %first_rows.1, ...), custom_call_target="tpu_custom_call" | custom-call | tf_op jit(solution)/shard_map/clipped_adam/pallas_call | solution.py:423
  70.3 2.0 %scale.1 = (f32[256,1024]{1,0:T(8,128)}, f32[256,1024]{1,0:T(8,128)}, f32[256,1024]{1,0:T(8,128)}, f32[1,256]{1,0:T(1,128)}, f32[1,1024]{1,0:T(1,128)}, /*index=5*/f32[1,256]{1,0:T(1,128)}, f32[1,1024]{1,0:T(1,128)}) custom-call(f32[256,1024]{1,0:T(8,128)S(1)} %get-tuple-element.20.first_new, f32[256,1024]{1,0:T(8,128)S(1)} %get-tuple-element.21.second_new, ...), custom_call_target="tpu_custom_call" | custom-call | tf_op jit(solution)/shard_map/scale/pallas_call | solution.py:471

commit v5 on v4

--- a/solution.py
+++ b/solution.py
@@ -20,6 +20,7 @@
 scale_floor = 0.001
 
 SLICES = 8
+ACROSS = 2
 AHEAD = 3
 ROUNDS = 6
 TILES = 8
@@ -66,8 +67,10 @@
     own_sem, got_sem, code_sem, l_sem, m_sem, l2_sem, m2_sem, small_sem,
     got_send, sends, small_send, word_sem,
 ):
-    slices, _, _, rows, width = own.shape
-    quarter = width // 4
+    slices, *_, rows, span = own.shape
+    width = grad.shape[1]
+    across = width // span
+    quarter = span // 4
     y, z, c, x = (lax.axis_index(a) for a in (Y, Z, C, X))
     at = (y, z)
     names = (Y, Z)
@@ -80,19 +83,28 @@
     peers = [{C: other}]
     for axis, name in enumerate(names):
         for k in (1, 3):
-            peers.append({name: step(at[axis], k)})
+            peers.append({name: step(at[axis], k), C: other})
     for k in (1, 3):
         peers.append({X: step(x, k)})
     for peer in peers:
         pl.semaphore_signal(barrier, inc=1, device_id=peer, device_id_type=MESH)
 
-    half = pltpu.make_async_copy(grads.at[:, :, other, pl.ds(0, rows), :], gift, own_sem.at[2])
-    half.start()
+    def block(p):
+        down = pl.ds(pl.multiple_of(p // across * rows, rows), rows)
+        return down, pl.ds(pl.multiple_of(p % across * span, span), span)
+
+    def pieces(p, core):
+        for i in range(2):
+            for j in range(2):
+                whose = lax.rem(core + y + z + i + j, 2)
+                yield grads.at[:, i, :, j, whose, *block(p)], (slice(None), i, slice(None), j)
+
+    for piece, where in pieces(0, other):
+        pltpu.make_async_copy(piece, gift.at[where], own_sem.at[2]).start()
 
     def load(p, sem):
-        pltpu.make_async_copy(
-            grads.at[:, :, c, pl.ds(p * rows, rows), :], own.at[p], own_sem.at[sem]
-        ).start()
+        for piece, where in pieces(p, c):
+            pltpu.make_async_copy(piece, own.at[(p, *where)], own_sem.at[sem]).start()
         return sem
 
     load(0, 0)
@@ -120,17 +132,15 @@
                 )
 
     def give(p, _):
-        remote(
-            grads.at[:, :, other, pl.ds(p * rows, rows), :], got.at[p],
-            got_send, got_sem.at[p], {C: other},
-        ).start()
+        for piece, where in pieces(p, other):
+            remote(piece, got.at[(p, *where)], got_send, got_sem.at[p], {C: other}).start()
         return _
 
     halves = [pl.ds(0, 2 * quarter), pl.ds(2 * quarter, 2 * quarter)]
-    half.wait()
+    landed(gift, own_sem.at[2])
     for axis in (0, 1):
         remote(
-            gift.at[:, :, :, halves[axis]], got.at[0, :, :, :, halves[axis]],
+            gift.at[:, :, :, :, :, halves[axis]], got.at[0, :, :, :, :, :, halves[axis]],
             got_send, got_sem.at[axis * slices], {C: other},
         ).start()
     lax.fori_loop(1, AHEAD + 1, give, 0)
@@ -139,8 +149,9 @@
         return pl.ds((2 * axis + slot) * quarter, quarter)
 
     def pair(p, axis, index, j, slot):
-        where = (p, index, j) if axis == 0 else (p, j, index)
-        where = (*where, slice(None), columns(axis, slot))
+        index, j = (index // 2, index % 2), (j // 2, j % 2)
+        where = (*index, *j) if axis == 0 else (*j, *index)
+        where = (p, *where, slice(None), columns(axis, slot))
         return own[where].astype(jnp.float32) + got[where].astype(jnp.float32)
 
     def send(kind, key, ref, ref_t, out, out_t, sem, device):
@@ -164,12 +175,12 @@
                 values += [pair(p, axis, step(me, k), j, 1 - slot) for j in range(4)]
                 put(values, sent_l, sent_lt, (p, axis, slot))
                 send(0, (p, axis, slot), sent_l, sent_lt, came_l, came_lt, l_sem.at[p],
-                     {names[axis]: step(me, k)})
+                     {names[axis]: step(me, k), C: other})
 
     def first_ready(axis):
         if axis == 0:
             landed(own.at[0], own_sem.at[0])
-        landed(got.at[0, :, :, :, halves[axis]], got_sem.at[axis * slices])
+        landed(got.at[0, :, :, :, :, :, halves[axis]], got_sem.at[axis * slices])
 
     def later(p, _):
         leaves(p, lambda axis: None if axis else landed(got.at[p], got_sem.at[p]))
@@ -191,7 +202,7 @@
                 ]
                 put(values, sent_m, sent_mt, key)
                 send(1, key, sent_m, sent_mt, came_m, came_mt, m_sem.at[p],
-                     {names[axis]: step(me, k)})
+                     {names[axis]: step(me, k), C: other})
         return _
 
     def both(p, _):
@@ -221,7 +232,7 @@
     def totals(p, _):
         arrived(4, 4, m_sem.at[p])
         for axis in (0, 1):
-            me, over, across = at[axis], at[1 - axis], names[1 - axis]
+            me, over, way = at[axis], at[1 - axis], names[1 - axis]
             for slot, k in DIRS:
                 for j in range(4):
                     total[p, axis, slot, j] = (
@@ -236,7 +247,7 @@
                 ]
                 put(values, sent_l2, sent_l2t, (p, axis, slot))
                 send(2, (p, axis, slot), sent_l2, sent_l2t, came_l2, came_l2t, l2_sem.at[p],
-                     {across: step(over, k)})
+                     {way: step(over, k), C: other})
         return _
 
     lax.fori_loop(0, slices, totals, 0)
@@ -244,13 +255,13 @@
     def middles2(p, _):
         arrived(4, 2, l2_sem.at[p])
         for axis in (0, 1):
-            over, across = at[1 - axis], names[1 - axis]
+            over, way = at[1 - axis], names[1 - axis]
             for slot, k in DIRS:
                 key = (p, axis, slot)
                 value = total[p, axis, slot, step(over, k)] + take(came_l2, came_l2t, key, 0)
                 put([value], sent_m2, sent_m2t, key)
                 send(3, key, sent_m2, sent_m2t, came_m2, came_m2t, m2_sem.at[p],
-                     {across: step(over, k)})
+                     {way: step(over, k), C: other})
         return _
 
     lax.fori_loop(0, slices, middles2, 0)
@@ -267,7 +278,8 @@
                     + take(came_m2, came_m2t, (p, axis, slot), 0)
                     + take(came_l2, came_l2t, (p, axis, 1 - slot), 1)
                 )
-                grad[pl.ds(pl.multiple_of(p * rows, rows), rows), columns(axis, slot)] = value
+                here = pl.multiple_of(p % across * span + (2 * axis + slot) * quarter, quarter)
+                grad[block(p)[0], pl.ds(here, quarter)] = value
                 sq = value * value
                 part = sq[:, :128]
                 for j in range(1, quarter // 128):
@@ -308,11 +320,11 @@
         places.sort(key=lambda place: -sum(hops[k] for k in place))
         return [{X: step(x, kx), Y: step(y, ky), Z: step(z, kz)} for kx, ky, kz in places]
 
-    exchange(squares, norm_c, [{C: other}], 0)
-    landed(norm_c, small_sem.at[0])
-    landed(norm_c, small_send.at[0])
-    squares[...] += norm_c[0]
-    spread(squares, norm_p, far_first(range(4)), 1)
+    everyone = [
+        {**place, C: step2} for place in far_first(range(4)) for step2 in (c, other)
+    ] + [{C: other}]
+    exchange(squares, norm_p, everyone, 1)
+    landed(norm_p, small_sem.at[1])
     square_sum = jnp.sum(squares[...] + jnp.sum(norm_p[...], axis=0), keepdims=True)
     clip_scale = clip_limit / jnp.maximum(jnp.sqrt(square_sum), clip_limit)
 
@@ -352,7 +364,7 @@
     result = jnp.maximum(colmax[...], jnp.max(col_z[...], axis=0))
     first_colmax[...] = jnp.maximum(result[0:1], scale_floor)
     second_colmax[...] = result[1:2]
-    spread_done(norm_p, 1)
+    landed(norm_p, small_send.at[1])
     spread_done(col_z, 3)
 
     landed(got, got_send)
@@ -406,13 +418,14 @@
     entries = layer_count * lax.axis_size(X) * row_count * col_count
     clip_limit = clip_rms * math.sqrt(entries)
     own_rows = first_codes.shape[1]
-    rows = own_rows // SLICES
-    q = col_count // 4
+    rows = own_rows * ACROSS // SLICES
+    span = col_count // ACROSS
+    q = span // 4
     f32, bf16 = jnp.float32, jnp.bfloat16
     shape = jax.ShapeDtypeStruct
     vmem = pltpu.VMEM
     dma = pltpu.SemaphoreType.DMA
-    grads = grad_parts.reshape(4, 4, 2, own_rows, col_count)
+    grads = grad_parts.reshape(2, 2, 2, 2, 2, own_rows, col_count)
     hbm_spec = pl.BlockSpec(memory_space=pltpu.HBM)
     vmem_spec = pl.BlockSpec(memory_space=pltpu.VMEM)
     n = SLICES
@@ -430,8 +443,8 @@
         in_specs=[hbm_spec] * 7,
         out_specs=[vmem_spec] * 6,
         scratch_shapes=[
-            vmem((n, 4, 4, rows, col_count), bf16),
-            vmem((n, 4, 4, rows, col_count), bf16),
+            vmem((n, 2, 2, 2, 2, rows, span), bf16),
+            vmem((n, 2, 2, 2, 2, rows, span), bf16),
             *coded(8), *coded(8),
             *coded(4), *coded(4),
             vmem((n, 2, 2, 4, rows, q), f32),
@@ -442,14 +455,14 @@
             vmem((8, 128), f32),
             vmem((1, 128), f32),
             vmem((1, 1, 128), f32),
-            vmem((63, 1, 128), f32),
+            vmem((127, 1, 128), f32),
             vmem((2, own_rows, 128), f32),
             vmem((2, col_count), f32),
             vmem((1, 2, col_count), f32),
             vmem((15, 2, col_count), f32),
             *[vmem((1, own_rows), f32), vmem((1, col_count), f32)] * 2,
             vmem((1, 16 * (rows + 1) * q), f32),
-            vmem((4, 4, rows, col_count), bf16),
+            vmem((2, 2, 2, 2, rows, span), bf16),
             dma((3,)), dma((n + 1,)), dma((2,)),
             dma((n,)), dma((n,)), dma((n,)), dma((n,)), dma((4,)),
             dma, dma((8,)), dma((4,)), pltpu.SemaphoreType.REGULAR((ROUNDS,)),

time: 72.4 us -> 71.5 us (0.988)
  Pallas kernels: 71.7 us -> 70.7 us
    pallas_call x1, Pallas kernels: 69.7 us -> 68.7 us  [local(): pl.pallas_call(functools.partial(kernel, clip_limit), out_shape=(shape((o...]
where the time goes in v5:
time: 71.5 us; the launch traced here: 71.4 us
  Pallas kernels  70.7 us (99%)
    pallas_call x1, Pallas kernels, local(): pl.pallas_call(functools.partial(kernel, clip_limit), out_shape=(shape((o...  68.7 us
    pallas_call x1, Pallas kernels, local(): pl.pallas_call(scale, out_shape=(big, big, big, by_row, by_col, by_row, b...  2.02 us

profile of v5, /device:TPU:1, one launch (start us, length us, event | category | flops | bytes accessed | tf_op | source)
XLA Modules:
  0.0 71.4 jit_solution(10861814269188662806)
XLA Ops:
  0.6 68.7 %clipped_adam.1 = (f32[256,1024]{1,0:T(8,128)S(1)}, f32[256,1024]{1,0:T(8,128)S(1)}, f32[1,256]{1,0:T(1,128)S(1)}, f32[1,1024]{1,0:T(1,128)S(1)}, f32[1,256]{1,0:T(1,128)S(1)}, /*index=5*/f32[1,1024]{1,0:T(1,128)S(1)}) custom-call(bf16[2,2,2,2,2,256,1024]{6,5,4,3,2,1,0:T(8,128)(2,1)} %bitcast.6, s32[256,1024]{1,0:T(8,128)} %bitcast.7, f32[1,256]{1,0:T(1,128)} %first_rows.1, ...), custom_call_target="tpu_custom_call" | custom-call | tf_op jit(solution)/shard_map/clipped_adam/pallas_call | solution.py:436
  69.4 2.0 %scale.1 = (f32[256,1024]{1,0:T(8,128)}, f32[256,1024]{1,0:T(8,128)}, f32[256,1024]{1,0:T(8,128)}, f32[1,256]{1,0:T(1,128)}, f32[1,1024]{1,0:T(1,128)}, /*index=5*/f32[1,256]{1,0:T(1,128)}, f32[1,1024]{1,0:T(1,128)}) custom-call(f32[256,1024]{1,0:T(8,128)S(1)} %get-tuple-element.20.first_new, f32[256,1024]{1,0:T(8,128)S(1)} %get-tuple-element.21.second_new, ...), custom_call_target="tpu_custom_call" | custom-call | tf_op jit(solution)/shard_map/scale/pallas_call | solution.py:484

commit v6 on v5

--- a/solution.py
+++ b/solution.py
@@ -23,7 +23,7 @@
 ACROSS = 2
 AHEAD = 3
 ROUNDS = 6
-TILES = 8
+TILES = 4
 LEVELS = 32766.0
 TINY = 2e-34
 DIRS = ((0, 1), (1, 3))
@@ -59,7 +59,7 @@
 def kernel(
     clip_limit,
     grads, first_codes, first_rows, first_columns, second_codes, second_rows, second_columns,
-    first_new, second_new, first_rowmax, first_colmax, second_rowmax, second_colmax,
+    direction, first_new, second_new, first_rowmax, first_colmax, second_rowmax, second_colmax,
     own, got, sent_l, sent_lt, came_l, came_lt, sent_m, sent_mt, came_m, came_mt, total,
     sent_l2, sent_l2t, came_l2, came_l2t, sent_m2, sent_m2t, came_m2, came_m2t,
     codes, grad, sums, squares, norm_c, norm_p, rowmax, colmax, col_c, col_z,
@@ -136,17 +136,34 @@
             remote(piece, got.at[(p, *where)], got_send, got_sem.at[p], {C: other}).start()
         return _
 
-    halves = [pl.ds(0, 2 * quarter), pl.ds(2 * quarter, 2 * quarter)]
+    def columns(axis, slot):
+        return pl.ds((2 * axis + slot) * quarter, quarter)
+
+    def block_of(axis, index, slot):
+        where = (index // 2, index % 2)
+        around = (slice(None), slice(None))
+        where = (*where, *around) if axis == 0 else (*around, *where)
+        return (*where, slice(None), columns(axis, slot))
+
+    def gift_block(axis, index, slot, sem):
+        where = block_of(axis, index, slot)
+        remote(
+            gift.at[where], got.at[(0, *where)], got_send, got_sem.at[sem], {C: other}
+        ).start()
+
     landed(gift, own_sem.at[2])
     for axis in (0, 1):
-        remote(
-            gift.at[:, :, :, :, :, halves[axis]], got.at[0, :, :, :, :, :, halves[axis]],
-            got_send, got_sem.at[axis * slices], {C: other},
-        ).start()
+        for slot, k in DIRS:
+            gift_block(axis, step(at[axis], 2), slot, slices + 2 * axis + slot)
+            gift_block(axis, step(at[axis], k), 1 - slot, slices + 2 * axis + slot)
+    for axis in (0, 1):
+        for slot, k in DIRS:
+            gift_block(axis, step(at[axis], k), slot, 0)
+            gift_block(axis, at[axis], slot, 0)
     lax.fori_loop(1, AHEAD + 1, give, 0)
 
-    def columns(axis, slot):
-        return pl.ds((2 * axis + slot) * quarter, quarter)
+    def blocks_landed(count, sem):
+        landed(words_ref.at[:, pl.ds(0, count * 4 * rows * quarter // 2)], sem)
 
     def pair(p, axis, index, j, slot):
         index, j = (index // 2, index % 2), (j // 2, j % 2)
@@ -169,25 +186,30 @@
 
         for axis in (0, 1):
             me = at[axis]
-            ready(axis)
             for slot, k in DIRS:
+                ready(axis, slot)
                 values = [pair(p, axis, step(me, 2), j, slot) for j in range(4)]
                 values += [pair(p, axis, step(me, k), j, 1 - slot) for j in range(4)]
                 put(values, sent_l, sent_lt, (p, axis, slot))
                 send(0, (p, axis, slot), sent_l, sent_lt, came_l, came_lt, l_sem.at[p],
                      {names[axis]: step(me, k), C: other})
 
-    def first_ready(axis):
-        if axis == 0:
+    def first_ready(axis, slot):
+        if axis == 0 and slot == 0:
             landed(own.at[0], own_sem.at[0])
-        landed(got.at[0, :, :, :, :, :, halves[axis]], got_sem.at[axis * slices])
+        blocks_landed(2, got_sem.at[slices + 2 * axis + slot])
+
+    def later_ready(p, axis, slot):
+        if axis == 0 and slot == 0:
+            landed(got.at[p], got_sem.at[p])
 
     def later(p, _):
-        leaves(p, lambda axis: None if axis else landed(got.at[p], got_sem.at[p]))
+        leaves(p, functools.partial(later_ready, p))
         return _
 
     leaves(0, first_ready)
     landed(own.at[pl.ds(1, slices - 1)], own_sem.at[1])
+    blocks_landed(8, got_sem.at[0])
     lax.fori_loop(1, AHEAD, later, 0)
 
     def middles(p, _):
@@ -294,7 +316,7 @@
         for i, target in enumerate(targets):
             remote(value_ref, slots.at[i], small_send.at[sem], small_sem.at[sem], target).start()
 
-    def spread(value_ref, slots, places, sem):
+    def send_spread(value_ref, slots, places, sem):
         @pl.when(c == 1)
         def _send():
             for i, place in enumerate(places):
@@ -303,8 +325,6 @@
                         value_ref, slots.at[i], small_send.at[sem], small_sem.at[sem],
                         {**place, C: core},
                     ).start()
-
-        landed(slots, small_sem.at[sem])
 
     def spread_done(slots, sem):
         @pl.when(c == 1)
@@ -360,7 +380,15 @@
     landed(col_c, small_sem.at[2])
     landed(col_c, small_send.at[2])
     colmax[...] = jnp.maximum(colmax[...], col_c[0])
-    spread(colmax, col_z, far_first((0,)), 3)
+    send_spread(colmax, col_z, far_first((0,)), 3)
+
+    def direct(t, _):
+        here = pl.ds(pl.multiple_of(t * tile, tile), tile)
+        direction[here, :] = first_new[here, :] / (jnp.sqrt(second_new[here, :]) + epsilon)
+        return _
+
+    lax.fori_loop(0, grad.shape[0] // tile, direct, 0)
+    landed(col_z, small_sem.at[3])
     result = jnp.maximum(colmax[...], jnp.max(col_z[...], axis=0))
     first_colmax[...] = jnp.maximum(result[0:1], scale_floor)
     second_colmax[...] = result[1:2]
@@ -376,13 +404,14 @@
 
 
 def scale(
-    first_new, second_new, first_rowmax, first_colmax, second_rowmax, second_colmax,
-    direction, first_scaled, second_scaled,
+    direction, first_new, second_new, first_rowmax, first_colmax, second_rowmax, second_colmax,
+    direction_out, first_scaled, second_scaled,
     first_row_out, first_col_out, second_row_out, second_col_out,
     out, out_sem, max_sem,
 ):
     copies = [
         pltpu.make_async_copy(ref, to, max_sem.at[i]) for i, (ref, to) in enumerate((
+            (direction, direction_out),
             (first_rowmax, first_row_out), (first_colmax, first_col_out),
             (second_rowmax, second_row_out), (second_colmax, second_col_out),
         ))
@@ -391,19 +420,17 @@
         copy.start()
     rows, width = first_new.shape
     tile = rows // TILES
-    by_row = [
-        jnp.transpose(jnp.broadcast_to(ref[...], (128, rows)))
-        for ref in (first_rowmax, second_rowmax)
-    ]
-    for t in range(TILES):
-        here = slice(t * tile, (t + 1) * tile)
-        for j in range(width // 128):
-            cols = slice(j * 128, j * 128 + 128)
-            first, second = first_new[here, cols], second_new[here, cols]
-            out[0, here, cols] = first / (jnp.sqrt(second) + epsilon)
-            out[1, here, cols] = first / jnp.minimum(by_row[0][here], first_colmax[:, cols])
-            out[2, here, cols] = second / jnp.minimum(by_row[1][here], second_colmax[:, cols])
-        for i, to in enumerate((direction, first_scaled, second_scaled)):
+    for i, (value, row, col, to) in enumerate((
+        (first_new, first_rowmax, first_colmax, first_scaled),
+        (second_new, second_rowmax, second_colmax, second_scaled),
+    )):
+        by_row = jnp.transpose(jnp.broadcast_to(1.0 / row[...], (128, rows)))
+        by_col = 1.0 / col[...]
+        for t in range(TILES):
+            here = slice(t * tile, (t + 1) * tile)
+            for j in range(width // 128):
+                cols = slice(j * 128, j * 128 + 128)
+                out[i, here, cols] = value[here, cols] * jnp.maximum(by_row[here], by_col[:, cols])
             copy = pltpu.make_async_copy(out.at[i, here], to.at[here], out_sem.at[t, i])
             copy.start()
             copies.append(copy)
@@ -433,15 +460,15 @@
     def coded(count):
         return vmem((n, 2, 2, count, rows, q), jnp.int16), vmem((n, 2, 2, count, q), bf16 if count > 1 else f32)
 
-    first_new, second_new, first_rowmax, first_colmax, second_rowmax, second_colmax = pl.pallas_call(
+    results = pl.pallas_call(
         functools.partial(kernel, clip_limit),
         out_shape=(
-            shape((own_rows, col_count), f32), shape((own_rows, col_count), f32),
+            *[shape((own_rows, col_count), f32)] * 3,
             shape((1, own_rows), f32), shape((1, col_count), f32),
             shape((1, own_rows), f32), shape((1, col_count), f32),
         ),
         in_specs=[hbm_spec] * 7,
-        out_specs=[vmem_spec] * 6,
+        out_specs=[vmem_spec] * 7,
         scratch_shapes=[
             vmem((n, 2, 2, 2, 2, rows, span), bf16),
             vmem((n, 2, 2, 2, 2, rows, span), bf16),
@@ -463,7 +490,7 @@
             *[vmem((1, own_rows), f32), vmem((1, col_count), f32)] * 2,
             vmem((1, 16 * (rows + 1) * q), f32),
             vmem((2, 2, 2, 2, rows, span), bf16),
-            dma((3,)), dma((n + 1,)), dma((2,)),
+            dma((3,)), dma((n + 4,)), dma((2,)),
             dma((n,)), dma((n,)), dma((n,)), dma((n,)), dma((4,)),
             dma, dma((8,)), dma((4,)), pltpu.SemaphoreType.REGULAR((ROUNDS,)),
         ],
@@ -484,12 +511,12 @@
     direction, first_scaled, second_scaled, *maxima = pl.pallas_call(
         scale,
         out_shape=(big, big, big, by_row, by_col, by_row, by_col),
-        in_specs=[vmem_spec] * 6,
+        in_specs=[vmem_spec] * 7,
         out_specs=[hbm_spec] * 7,
-        scratch_shapes=[vmem((3, own_rows, col_count), f32), dma((TILES, 3)), dma((4,))],
+        scratch_shapes=[vmem((2, own_rows, col_count), f32), dma((TILES, 2)), dma((5,))],
         compiler_params=pltpu.CompilerParams(vmem_limit_bytes=12 * 2**20),
         name="scale",
-    )(first_new, second_new, first_rowmax, first_colmax, second_rowmax, second_colmax)
+    )(*results)
     return direction[None], first_scaled[None], second_scaled[None], *maxima
 
 

time: 71.5 us -> 70.1 us (0.980)
  Pallas kernels: 70.7 us -> 69.4 us
    pallas_call x1, Pallas kernels: 68.7 us -> 67.6 us  [local(): pl.pallas_call(functools.partial(kernel, clip_limit), out_shape=(*[shape(...]
where the time goes in v6:
time: 70.1 us; the launch traced here: 70 us
  Pallas kernels  69.4 us (99%)
    pallas_call x1, Pallas kernels, local(): pl.pallas_call(functools.partial(kernel, clip_limit), out_shape=(*[shape(...  67.6 us
    pallas_call x1, Pallas kernels, local(): pl.pallas_call(scale, out_shape=(big, big, big, by_row, by_col, by_row, b...  1.79 us

profile of v6, /device:TPU:1, one launch (start us, length us, event | category | flops | bytes accessed | tf_op | source)
XLA Modules:
  0.0 70.0 jit_solution(6027209043457137806)
XLA Ops:
  0.6 67.6 %clipped_adam.1 = (f32[256,1024]{1,0:T(8,128)S(1)}, f32[256,1024]{1,0:T(8,128)S(1)}, f32[256,1024]{1,0:T(8,128)S(1)}, f32[1,256]{1,0:T(1,128)S(1)}, f32[1,1024]{...) custom-call(bf16[2,2,2,2,2,256,1024]{6,5,4,3,2,1,0:T(8,128)(2,1)} %bitcast.6, s32[256,1024]{1,0:T(8,128)} %bitcast.7, ...), custom_call_target="tpu_custom_call" | custom-call | tf_op jit(solution)/shard_map/clipped_adam/pallas_call | solution.py:463
  68.2 1.8 %scale.1 = (f32[256,1024]{1,0:T(8,128)}, f32[256,1024]{1,0:T(8,128)}, f32[256,1024]{1,0:T(8,128)}, f32[1,256]{1,0:T(1,128)}, f32[1,1024]{1,0:T(1,128)}, /*index=5*/f32[1,256]{1,0:T(1,128)}, f32[1,1024]{1,0:T(1,128)}) custom-call(f32[256,1024]{1,0:T(8,128)S(1)} %get-tuple-element.21.direction, f32[256,1024]{1,0:T(8,128)S(1)} %get-tuple-element.22.first_new, ...), custom_call_target="tpu_custom_call" | custom-call | tf_op jit(solution)/shard_map/scale/pallas_call | solution.py:511

commit v7 on v6

--- a/solution.py
+++ b/solution.py
@@ -349,51 +349,62 @@
     clip_scale = clip_limit / jnp.maximum(jnp.sqrt(square_sum), clip_limit)
 
     tile = 32
-    first_top = jnp.zeros((8, width), jnp.float32)
-    second_top = jnp.zeros((8, width), jnp.float32)
-
-    def moment(t, tops):
-        here = pl.ds(pl.multiple_of(t * tile, tile), tile)
-        clipped = clip_scale * grad[here, :]
-        first = first_new[here, :] + (1.0 - beta_first) * clipped
-        second = second_new[here, :] + (1.0 - beta_second) * clipped * clipped
-        first_new[here, :] = first
-        second_new[here, :] = second
-        outs = []
-        for i, (value, top) in enumerate(((jnp.abs(first), tops[0]), (second, tops[1]))):
-            outs.append(jnp.maximum(top, jnp.max(value.reshape(tile // 8, 8, width), axis=0)))
+    tiles = grad.shape[0] // tile
+    half = width // 2
+
+    def rows_of(t):
+        return pl.ds(pl.multiple_of(t * tile, tile), tile)
+
+    for h in range(2):
+        cols = pl.ds(h * half, half)
+
+        def moment(t, tops, cols=cols):
+            here = rows_of(t)
+            clipped = clip_scale * grad[here, cols]
+            first = first_new[here, cols] + (1.0 - beta_first) * clipped
+            second = second_new[here, cols] + (1.0 - beta_second) * clipped * clipped
+            first_new[here, cols] = first
+            second_new[here, cols] = second
+            return tuple(
+                jnp.maximum(top, jnp.max(value.reshape(tile // 8, 8, half), axis=0))
+                for value, top in ((jnp.abs(first), tops[0]), (second, tops[1]))
+            )
+
+        tops = lax.fori_loop(0, tiles, moment, (jnp.zeros((8, half), jnp.float32),) * 2)
+        for i in range(2):
+            colmax[h, i : i + 1, :] = jnp.max(tops[i], axis=0, keepdims=True)
+        exchange(colmax.at[h], col_c.at[h], [{C: other}], 2 + h)
+
+    for h in range(2):
+        landed(col_c.at[h], small_sem.at[2 + h])
+        landed(col_c.at[h], small_send.at[2 + h])
+        colmax[h] = jnp.maximum(colmax[h], col_c[h, 0])
+        send_spread(colmax.at[h], col_z.at[h], far_first((0,)), 4 + h)
+
+    def direct(t, _):
+        here = rows_of(t)
+        first, second = first_new[here, :], second_new[here, :]
+        direction[here, :] = first / (jnp.sqrt(second) + epsilon)
+        for i, value in enumerate((jnp.abs(first), second)):
             most = value[:, :128]
             for j in range(1, width // 128):
                 most = jnp.maximum(most, value[:, j * 128 : (j + 1) * 128])
             rowmax[i, here, :] = most
-        return tuple(outs)
-
-    first_top, second_top = lax.fori_loop(0, grad.shape[0] // tile, moment, (first_top, second_top))
-    colmax[0:1, :] = jnp.max(first_top, axis=0, keepdims=True)
-    colmax[1:2, :] = jnp.max(second_top, axis=0, keepdims=True)
-
-    exchange(colmax, col_c, [{C: other}], 2)
+        return _
+
+    lax.fori_loop(0, tiles, direct, 0)
     first_row = jnp.max(jnp.transpose(rowmax[0]), axis=0, keepdims=True)
     first_rowmax[...] = jnp.maximum(first_row, scale_floor)
     second_rowmax[...] = jnp.max(jnp.transpose(rowmax[1]), axis=0, keepdims=True)
 
-    landed(col_c, small_sem.at[2])
-    landed(col_c, small_send.at[2])
-    colmax[...] = jnp.maximum(colmax[...], col_c[0])
-    send_spread(colmax, col_z, far_first((0,)), 3)
-
-    def direct(t, _):
-        here = pl.ds(pl.multiple_of(t * tile, tile), tile)
-        direction[here, :] = first_new[here, :] / (jnp.sqrt(second_new[here, :]) + epsilon)
-        return _
-
-    lax.fori_loop(0, grad.shape[0] // tile, direct, 0)
-    landed(col_z, small_sem.at[3])
-    result = jnp.maximum(colmax[...], jnp.max(col_z[...], axis=0))
-    first_colmax[...] = jnp.maximum(result[0:1], scale_floor)
-    second_colmax[...] = result[1:2]
+    for h in range(2):
+        landed(col_z.at[h], small_sem.at[4 + h])
+        result = jnp.maximum(colmax[h], jnp.max(col_z[h], axis=0))
+        first_colmax[:, h * half : (h + 1) * half] = jnp.maximum(result[0:1], scale_floor)
+        second_colmax[:, h * half : (h + 1) * half] = result[1:2]
     landed(norm_p, small_send.at[1])
-    spread_done(col_z, 3)
+    for h in range(2):
+        spread_done(col_z.at[h], 4 + h)
 
     landed(got, got_send)
     for kind, (ref, ref_t) in enumerate((
@@ -484,15 +495,15 @@
             vmem((1, 1, 128), f32),
             vmem((127, 1, 128), f32),
             vmem((2, own_rows, 128), f32),
-            vmem((2, col_count), f32),
-            vmem((1, 2, col_count), f32),
-            vmem((15, 2, col_count), f32),
+            vmem((2, 2, col_count // 2), f32),
+            vmem((2, 1, 2, col_count // 2), f32),
+            vmem((2, 15, 2, col_count // 2), f32),
             *[vmem((1, own_rows), f32), vmem((1, col_count), f32)] * 2,
             vmem((1, 16 * (rows + 1) * q), f32),
             vmem((2, 2, 2, 2, rows, span), bf16),
             dma((3,)), dma((n + 4,)), dma((2,)),
-            dma((n,)), dma((n,)), dma((n,)), dma((n,)), dma((4,)),
-            dma, dma((8,)), dma((4,)), pltpu.SemaphoreType.REGULAR((ROUNDS,)),
+            dma((n,)), dma((n,)), dma((n,)), dma((n,)), dma((6,)),
+            dma, dma((8,)), dma((6,)), pltpu.SemaphoreType.REGULAR((ROUNDS,)),
         ],
         compiler_params=pltpu.CompilerParams(
             collective_id=0, has_side_effects=True, vmem_limit_bytes=46 * 2**20

time: 70.1 us -> 70.1 us (level)
  no operation moved by 1% of the time
where the time goes in v7:
time: 70.1 us; the launch traced here: 70 us
  Pallas kernels  69.3 us (99%)
    pallas_call x1, Pallas kernels, local(): pl.pallas_call(functools.partial(kernel, clip_limit), out_shape=(*[shape(...  67.6 us
    pallas_call x1, Pallas kernels, local(): pl.pallas_call(scale, out_shape=(big, big, big, by_row, by_col, by_row, b...  1.79 us

profile of v7, /device:TPU:1, one launch (start us, length us, event | category | flops | bytes accessed | tf_op | source)
XLA Modules:
  0.0 70.0 jit_solution(8315478500607586627)
XLA Ops:
  0.6 67.6 %clipped_adam.1 = (f32[256,1024]{1,0:T(8,128)S(1)}, f32[256,1024]{1,0:T(8,128)S(1)}, f32[256,1024]{1,0:T(8,128)S(1)}, f32[1,256]{1,0:T(1,128)S(1)}, f32[1,1024]{...) custom-call(bf16[2,2,2,2,2,256,1024]{6,5,4,3,2,1,0:T(8,128)(2,1)} %bitcast.6, s32[256,1024]{1,0:T(8,128)} %bitcast.7, ...), custom_call_target="tpu_custom_call" | custom-call | tf_op jit(solution)/shard_map/clipped_adam/pallas_call | solution.py:474
  68.2 1.8 %scale.1 = (f32[256,1024]{1,0:T(8,128)}, f32[256,1024]{1,0:T(8,128)}, f32[256,1024]{1,0:T(8,128)}, f32[1,256]{1,0:T(1,128)}, f32[1,1024]{1,0:T(1,128)}, /*index=5*/f32[1,256]{1,0:T(1,128)}, f32[1,1024]{1,0:T(1,128)}) custom-call(f32[256,1024]{1,0:T(8,128)S(1)} %get-tuple-element.21.direction, f32[256,1024]{1,0:T(8,128)S(1)} %get-tuple-element.22.first_new, ...), custom_call_target="tpu_custom_call" | custom-call | tf_op jit(solution)/shard_map/scale/pallas_call | solution.py:522
